TPU v7x, 256 devices: a whole 4x4x8 slice. The times are simulated.
256 devices in a mesh: seq: 64 (over z, y, core), batch: 4 (over x).
Axes of the slice: x: 4, y: 4, z: 8, core: 2. Of those that a mesh axis runs over, the one named last changes fastest.
Arguments:
- queries: bfloat16 [4, 32768, 16, 128], P('batch', 'seq'), may hold values from -5 to 5
- keys: bfloat16 [4, 32768, 16, 128], P('batch', 'seq'), may hold values from -5 to 5
- values: bfloat16 [4, 32768, 16, 128], P('batch', 'seq'), may hold values from -5 to 5
- keep_count: int32 [4, 16, 256], P('batch'), may hold values from 0 to 128
- query_map: bfloat16 [16, 128, 8], replicated, may hold values from -0.5 to 0.5
- key_map: bfloat16 [16, 128, 8], replicated, may hold values from -0.5 to 0.5
- cotangent: bfloat16 [4, 32768, 16, 128], P('batch', 'seq'), may hold values from -5 to 5
Outputs:
- attended: bfloat16 [4, 32768, 16, 128], P('batch', 'seq')
- grad_query_map: float32 [16, 128, 8], replicated
- grad_key_map: float32 [16, 128, 8], replicated
All inputs are finite; a program needn't handle non-finite values.
Results may differ from a plain program's by a relative error of at most 0.0035.
Values may be sent and summed in bfloat16 or wider, within the bound.
No kernel may reach another device: no remote copies, remote signals or barrier semaphores. Data moves between devices by JAX's collectives and lax.ppermute only.
A program may use at most 128 MiB of HBM per device.

v0:
```python
import functools
import math

import jax
import jax.numpy as jnp
from jax import lax
from jax.experimental import pallas as pl
from jax.experimental.pallas import tpu as pltpu
from jax.sharding import Mesh
from jax.sharding import PartitionSpec as P

TILE = 128
HEADS = 16
RANK = 8
DH = 128
ROWS = HEADS * RANK
SEQ = ("z", "y", "core")
ALL = ("z", "y", "core", "batch")
SHIFT = 1.5
SCALE = 1.0 / math.sqrt(DH)
SCALE_LOG2 = SCALE * math.log2(math.e)
NEG = -1e30
F32 = jnp.float32
BF16 = jnp.bfloat16
NT = (((1,), (1,)), ((), ()))
TN = (((0,), (0,)), ((), ()))
NN = (((1,), (0,)), ((), ()))


def dot(a, b, dims=NN):
    return lax.dot_general(a, b, dims, preferred_element_type=F32)


def halves(x):
    hi = x.astype(BF16)
    return hi, (x - hi.astype(F32)).astype(BF16)


def stacked(x):
    hi = x.astype(BF16).astype(F32)
    return jnp.concatenate([hi, x - hi], 0).astype(BF16)


def folded(x):
    return x[:RANK] + x[RANK : 2 * RANK]


def row_sums(x):
    ones = jnp.ones((8, 128), BF16)
    hi, lo = halves(x)
    return dot(ones, hi, NT) + dot(ones, lo, NT)


def softplus_sigmoid(pre):
    e = jnp.exp(-jnp.abs(pre))
    value = jnp.maximum(pre, 0.0) + jnp.log1p(e)
    inv = 1.0 / (1.0 + e)
    return value, jnp.where(pre >= 0, inv, e * inv)


def per_head_sum(x):
    x = x.reshape(HEADS, RANK, TILE)
    x = jnp.broadcast_to(jnp.sum(x, 1, keepdims=True), x.shape)
    return x.reshape(ROWS, TILE)


def head_rows(h):
    return pl.ds(h * RANK, RANK)


def lane(x, k):
    at = lax.broadcasted_iota(jnp.int32, x.shape, 1) == k
    return jnp.sum(jnp.where(at, x, 0.0), 1, keepdims=True)


def keys_kernel(idx_ref, cnt_ref, k_ref, v_ref, kmap_ref, kh_ref, vh_ref, local_ref,
                sig_ref, evict_ref, nloc_ref, msg_ref, kscr, vscr, pre, all_acc, nacc, feats):
    n = pl.program_id(0)

    @pl.when(n == 0)
    def _():
        all_acc[...] = jnp.zeros_like(all_acc)
        nacc[...] = jnp.zeros_like(nacc)

    kscr[...] = k_ref[0].reshape(TILE * HEADS, DH).astype(F32)
    vscr[...] = v_ref[0].reshape(TILE * HEADS, DH).astype(F32)
    lanes = lax.broadcasted_iota(jnp.int32, (RANK, TILE), 1)
    for h in range(HEADS):
        kh = kscr[pl.ds(h, TILE, stride=HEADS), :].astype(BF16)
        kh_ref[h] = kh
        vh_ref[h] = vscr[pl.ds(h, TILE, stride=HEADS), :].astype(BF16)
        pre[head_rows(h), :] = dot(kmap_ref[h], kh, NT)
        count = cnt_ref[h, idx_ref[0] * 4 + n]
        evict_ref[0, head_rows(h), :] = (lanes >= count).astype(F32)
    feat, sig = softplus_sigmoid(pre[...] - SHIFT)
    sig_ref[0] = sig
    ev = feat * evict_ref[0]
    feats[0] = feat
    feats[1] = ev
    for h in range(HEADS):
        lhs = jnp.concatenate(
            [stacked(feats[0, head_rows(h), :]), stacked(feats[1, head_rows(h), :])], 0
        )
        res = dot(lhs, vh_ref[h])
        before = all_acc[head_rows(h), :]
        local_ref[0, head_rows(h), :] = before_last(before, folded(res[2 * RANK :]), n)
        all_acc[head_rows(h), :] = before + folded(res)
    all_norm = jnp.sum(feat, 1, keepdims=True)
    ev_norm = jnp.sum(ev, 1, keepdims=True)
    nloc_ref[0] = jnp.broadcast_to(ev_norm, (ROWS, TILE)) + nacc[...]
    nacc[...] += jnp.broadcast_to(all_norm, (ROWS, TILE))

    @pl.when(n == 3)
    def _():
        row = row_sums(nacc[...] * (1.0 / 128.0))
        for s in range(64):
            msg_ref[s, 0:2, :] = all_acc[2 * s : 2 * s + 2, :]
            msg_ref[s, 2:4, :] = row[0:2]


def before_last(before, ev, n):
    return before + ev


def attend_kernel(idx_ref, cnt_ref, q_ref, c_ref, kh_ref, vh_ref, hk_ref, hv_ref, qmap_ref,
                  kmap_ref, nloc_ref, got_ref, qh_ref, ch_ref, numer_ref, stats_ref, dst_ref,
                  halo_k_ref, halo_v_ref, halo_ref, msg_ref,
                  qscr, cscr, pk, pv, pre, mx, den, cn, norm, cf, dacc):
    t = pl.program_id(0)
    index = idx_ref[0]
    lanes = lax.broadcasted_iota(jnp.int32, (RANK, TILE), 1)

    @pl.when(t == 0)
    def _():
        dacc[...] = jnp.zeros_like(dacc)
        run = jnp.zeros((2, 128), F32)
        nrun = jnp.zeros((1, 128), F32)
        for s in range(64):
            msg_ref[s, 0:2, :] = run
            run = run + got_ref[s, 0:2, :]
            nrun = nrun + jnp.where(s < index, got_ref[s, 2:3, :], 0.0)
        norm[...] = jnp.broadcast_to(nrun, (128, 128)).T
        qscr[...] = hk_ref[...].reshape(TILE * HEADS, DH).astype(F32)
        cscr[...] = hv_ref[...].reshape(TILE * HEADS, DH).astype(F32)
        for h in range(HEADS):
            kh = qscr[pl.ds(h, TILE, stride=HEADS), :].astype(BF16)
            vh = cscr[pl.ds(h, TILE, stride=HEADS), :].astype(BF16)
            pk[h] = kh
            pv[h] = vh
            halo_k_ref[h] = kh
            halo_v_ref[h] = vh
            pre[head_rows(h), :] = dot(kmap_ref[h], kh, NT)
            count = jnp.where(index > 0, cnt_ref[h, jnp.maximum(index * 4 - 1, 0)], 0)
            halo_ref[1, head_rows(h), :] = (lanes < count).astype(F32)
        feat, sig = softplus_sigmoid(pre[...] - SHIFT)
        feat = feat * halo_ref[1]
        halo_ref[1] = halo_ref[1] * sig
        cf[...] = feat
        for h in range(HEADS):
            halo_ref[0, head_rows(h), :] = folded(dot(stacked(cf[head_rows(h), :]), pv[h]))
        kept_norm = jnp.sum(feat, 1, keepdims=True)
        stats_ref[0, 5] = norm[...] - kept_norm

    @pl.when(t > 0)
    def _():
        stats_ref[0, 5] = norm[...] + nloc_ref[0]

    qscr[...] = q_ref[0].reshape(TILE * HEADS, DH).astype(F32)
    cscr[...] = c_ref[0].reshape(TILE * HEADS, DH).astype(F32)
    rows = lax.broadcasted_iota(jnp.int32, (TILE, TILE), 0)
    cols = lax.broadcasted_iota(jnp.int32, (TILE, TILE), 1)
    causal = rows <= cols
    for h in range(HEADS):
        qh = qscr[pl.ds(h, TILE, stride=HEADS), :].astype(BF16)
        ch = cscr[pl.ds(h, TILE, stride=HEADS), :].astype(BF16)
        qh_ref[h] = qh
        ch_ref[h] = ch
        pre[head_rows(h), :] = dot(qmap_ref[h], qh, NT)
        before = index * 4 + t - 1
        count = jnp.where(before >= 0, cnt_ref[h, jnp.maximum(before, 0)], 0)
        vp, vo = pv[h], vh_ref[h]
        s_prev = jnp.where(rows < count, dot(pk[h], qh, NT), NEG)
        s_own = jnp.where(causal, dot(kh_ref[h], qh, NT), NEG)
        top = jnp.max(jnp.maximum(s_prev, s_own), 0, keepdims=True)
        w_prev = jnp.exp2((s_prev - top) * SCALE_LOG2)
        w_own = jnp.exp2((s_own - top) * SCALE_LOG2)
        sums = jnp.sum(w_prev + w_own, 0, keepdims=True)
        b_prev, b_own = w_prev.astype(BF16), w_own.astype(BF16)
        numer_ref[h] = dot(b_prev, vp, TN) + dot(b_own, vo, TN)
        against = b_prev.astype(F32) * dot(vp, ch, NT) + b_own.astype(F32) * dot(vo, ch, NT)
        mx[head_rows(h), :] = jnp.broadcast_to(top, (RANK, TILE))
        den[head_rows(h), :] = jnp.broadcast_to(sums, (RANK, TILE))
        cn[head_rows(h), :] = jnp.broadcast_to(jnp.sum(against, 0, keepdims=True), (RANK, TILE))
    pk[...] = kh_ref[...]
    pv[...] = vh_ref[...]
    feat, sig = softplus_sigmoid(pre[...] - SHIFT)
    decay = jnp.exp(-(mx[...] * SCALE))
    total = den[...] + decay * per_head_sum(feat * stats_ref[0, 5])
    rinv = 1.0 / total
    coef = decay * rinv
    stats_ref[0, 0] = feat
    stats_ref[0, 1] = sig
    stats_ref[0, 2] = coef
    stats_ref[0, 3] = rinv
    stats_ref[0, 4] = cn[...] * rinv
    cf[...] = feat * coef
    for h in range(HEADS):
        d = folded(dot(stacked(cf[head_rows(h), :]), ch_ref[h]))
        dst_ref[0, head_rows(h), :] = d
        dacc[head_rows(h), :] += d

    @pl.when(t == 3)
    def _():
        for s in range(64):
            msg_ref[s, 2:4, :] = dacc[2 * s : 2 * s + 2, :]


def output_kernel(numer_ref, qh_ref, ch_ref, stats_ref, local_ref, halo_ref, got_ref, out_ref,
                  gq_ref, dn_ref, msg_ref, far, state, oscr, grad, cf, drow):
    t = pl.program_id(0)

    @pl.when(t == 0)
    def _():
        gq_ref[...] = jnp.zeros_like(gq_ref)
        drow[...] = jnp.zeros_like(drow)
        for s in range(64):
            far[2 * s : 2 * s + 2, :] = got_ref[s, 0:2, :]
        run = jnp.zeros((2, 128), F32)
        for s in reversed(range(64)):
            msg_ref[s, 0:2, :] = run
            run = run + got_ref[s, 2:4, :]
        state[...] = far[...] - halo_ref[0]

    @pl.when(t > 0)
    def _():
        state[...] = far[...] + local_ref[0]

    feat, sig, coef, rinv, cnr, norm = (stats_ref[0, i] for i in range(6))
    cf[...] = feat * coef
    sub = lax.broadcasted_iota(jnp.int32, (RANK, TILE), 0)
    ones = jnp.ones((RANK, DH), F32)
    zeros = jnp.zeros((RANK, DH), F32)
    for h in range(HEADS):
        s = state[head_rows(h), :]
        s_hi = s.astype(BF16).astype(F32)
        s_lo = s - s_hi
        grad[head_rows(h), :] = folded(
            dot(jnp.concatenate([s_hi, s_lo], 0).astype(BF16), ch_ref[h], NT)
        )
        c = cf[head_rows(h), :]
        c_hi = c.astype(BF16).astype(F32)
        r = stats_ref[0, 3, head_rows(h), :]
        r_hi = r.astype(BF16).astype(F32)
        r_mid = (r - r_hi).astype(BF16).astype(F32)
        pieces = jnp.where(sub == 0, r_hi, jnp.where(sub == 1, r_mid, jnp.where(sub == 2, r - r_hi - r_mid, 0.0)))
        lhs = jnp.concatenate([c_hi, c - c_hi, c_hi, pieces], 0).astype(BF16)
        rhs = jnp.concatenate(
            [
                jnp.concatenate([s_hi, s_hi, s_lo, zeros], 0),
                jnp.concatenate([zeros, zeros, zeros, ones], 0),
            ],
            1,
        ).astype(BF16)
        both = dot(lhs, rhs, TN)
        oscr[pl.ds(h, TILE, stride=HEADS), :] = numer_ref[h] * both[:, DH:] + both[:, :DH]
    out_ref[0] = oscr[...].astype(BF16).reshape(TILE, HEADS, DH)
    g = grad[...]
    along = cnr + per_head_sum(cf[...] * g)
    grad[...] = coef * (g - along * norm) * sig
    for h in range(HEADS):
        gq_ref[head_rows(h), :] += folded(dot(stacked(grad[head_rows(h), :]), qh_ref[h]))
    dn = -(cf[...] * along)
    dn_ref[0] = jnp.broadcast_to(jnp.sum(dn, 1, keepdims=True), (ROWS, TILE))
    drow[...] += row_sums(dn)

    @pl.when(t == 3)
    def _():
        for s in range(64):
            msg_ref[s, 2:4, :] = drow[0:2, :]


def key_grad_kernel(idx_ref, kh_ref, vh_ref, sig_ref, evict_ref, dst_ref, dn_ref, halo_k_ref,
                    halo_v_ref, halo_ref, got_ref, gq_ref, out_ref, acc, nacc, grad, ev):
    i = pl.program_id(0)
    n = 3 - i
    index = idx_ref[0]

    @pl.when(i == 0)
    def _():
        out_ref[:ROWS, :] = gq_ref[...]
        nrun = jnp.zeros((1, 128), F32)
        for s in range(64):
            acc[2 * s : 2 * s + 2, :] = got_ref[s, 0:2, :]
            nrun = nrun + jnp.where(s > index, got_ref[s, 2:3, :], 0.0)
        nacc[...] = jnp.broadcast_to(nrun, (128, 128)).T
        for h in range(HEADS):
            grad[head_rows(h), :] = folded(
                dot(stacked(dst_ref[0, head_rows(h), :]), halo_v_ref[h], NT)
            )
        grad[...] = -(grad[...] + dn_ref[0]) * halo_ref[1]
        for h in range(HEADS):
            out_ref[pl.ds(ROWS + h * RANK, RANK), :] = folded(
                dot(stacked(grad[head_rows(h), :]), halo_k_ref[h])
            )

    @pl.when(i >= 2)
    def _():
        acc[...] += dst_ref[jnp.minimum(n + 2, 3)]
        nacc[...] += dn_ref[jnp.minimum(n + 2, 3)]

    after = jnp.minimum(n + 1, 3)
    live = (n < 3).astype(F32)
    for h in range(HEADS):
        lhs = jnp.concatenate(
            [stacked(acc[head_rows(h), :]), stacked(dst_ref[after, head_rows(h), :] * live)], 0
        )
        res = dot(lhs, vh_ref[h], NT)
        grad[head_rows(h), :] = folded(res)
        ev[head_rows(h), :] = folded(res[2 * RANK :])
    near = ev[...] + dn_ref[after] * live
    grad[...] = (grad[...] + nacc[...] + evict_ref[0] * near) * sig_ref[0]
    for h in range(HEADS):
        out_ref[pl.ds(ROWS + h * RANK, RANK), :] += folded(
            dot(stacked(grad[head_rows(h), :]), kh_ref[h])
        )


def total_kernel(x_ref, o_ref):
    o_ref[...] = jnp.broadcast_to(jnp.sum(x_ref[...], 0, keepdims=True), o_ref.shape)


def sds(shape, dtype=F32):
    return jax.ShapeDtypeStruct(shape, dtype)


def whole(shape):
    return pl.BlockSpec(shape, lambda *_: (0,) * len(shape))


SMEM = pl.BlockSpec(memory_space=pltpu.SMEM)
MAPS = whole((HEADS, RANK, DH))
MSG = whole((64, 4, 128))
NAT = pl.BlockSpec((1, TILE, HEADS, DH), lambda t: (0, t, 0, 0))
BYHEAD = pl.BlockSpec((HEADS, TILE, DH), lambda t: (0, t, 0))
PART = pl.BlockSpec((1, ROWS, TILE), lambda t: (t, 0, 0))
PREV = pl.BlockSpec((1, ROWS, TILE), lambda t: (jnp.maximum(t - 1, 0), 0, 0))
STATS = pl.BlockSpec((1, 6, ROWS, TILE), lambda t: (t, 0, 0, 0))
HALO = whole((HEADS, TILE, DH))
BIG = sds((HEADS, 4 * TILE, DH), BF16)
PARTS = sds((4, ROWS, TILE))
SQ = pltpu.VMEM((ROWS, TILE), F32)
FLAT = pltpu.VMEM((TILE * HEADS, DH), F32)
MSG_T = sds((64, 4, 128))


def exchanged(x, axes):
    return lax.all_to_all(x, axes, split_axis=0, concat_axis=0, tiled=True)


def call(kernel, name, grid, in_specs, out_specs, out_shape, scratch):
    return pl.pallas_call(
        kernel,
        grid=(grid,),
        in_specs=in_specs,
        out_specs=out_specs,
        out_shape=out_shape,
        scratch_shapes=scratch,
        name=name,
        compiler_params=pltpu.CompilerParams(
            dimension_semantics=("arbitrary",), vmem_limit_bytes=40 * 2**20
        ),
    )


def body(queries, keys, values, keep_count, query_map, key_map, cotangent):
    count = lax.axis_size(SEQ)
    steps = [(i, i + 1) for i in range(count - 1)]
    halo_k = lax.ppermute(keys[0, 3 * TILE :], SEQ, steps)
    halo_v = lax.ppermute(values[0, 3 * TILE :], SEQ, steps)
    index = lax.axis_index(SEQ).astype(jnp.int32).reshape(1)
    counts = keep_count[0]
    qmap = query_map.transpose(0, 2, 1)
    kmap = key_map.transpose(0, 2, 1)

    kh, vh, local, sig_k, evict, nloc, msg = call(
        keys_kernel, "keys", 4,
        [SMEM, SMEM, NAT, NAT, MAPS],
        [BYHEAD, BYHEAD, PART, PART, PART, PART, MSG],
        [BIG, BIG, PARTS, PARTS, PARTS, PARTS, MSG_T],
        [FLAT, FLAT, SQ, SQ, SQ, pltpu.VMEM((2, ROWS, TILE), F32)],
    )(index, counts, keys, values, kmap)

    got = exchanged(msg, SEQ)

    qh, ch, numer, stats, dst, hk, hv, halo, msg = call(
        attend_kernel, "attend", 4,
        [SMEM, SMEM, NAT, NAT, BYHEAD, BYHEAD, HALO_NAT, HALO_NAT, MAPS, MAPS, PREV, MSG],
        [BYHEAD, BYHEAD, BYHEAD, STATS, PART, HALO, HALO, whole((2, ROWS, TILE)), MSG],
        [BIG, BIG, sds((HEADS, 4 * TILE, DH)), sds((4, 6, ROWS, TILE)), PARTS,
         sds((HEADS, TILE, DH), BF16), sds((HEADS, TILE, DH), BF16), sds((2, ROWS, TILE)), MSG_T],
        [FLAT, FLAT, pltpu.VMEM((HEADS, TILE, DH), BF16), pltpu.VMEM((HEADS, TILE, DH), BF16),
         SQ, SQ, SQ, SQ, SQ, SQ, SQ],
    )(index, counts, queries, cotangent, kh, vh, halo_k, halo_v, qmap, kmap, nloc, got)

    got = exchanged(msg, SEQ)

    out, gq, dn, msg = call(
        output_kernel, "output", 4,
        [BYHEAD, BYHEAD, BYHEAD, STATS, PREV, whole((2, ROWS, TILE)), MSG],
        [NAT, whole((ROWS, TILE)), PART, MSG],
        [sds((1, 4 * TILE, HEADS, DH), BF16), sds((ROWS, TILE)), PARTS, MSG_T],
        [SQ, SQ, FLAT, SQ, SQ, pltpu.VMEM((8, 128), F32)],
    )(numer, qh, ch, stats, local, halo, got)

    got = exchanged(msg, SEQ)

    back = lambda t: (0, 3 - t, 0)
    part = lambda t: (3 - t, 0, 0)
    grads = call(
        key_grad_kernel, "key_grad", 4,
        [SMEM, pl.BlockSpec((HEADS, TILE, DH), back), pl.BlockSpec((HEADS, TILE, DH), back),
         pl.BlockSpec((1, ROWS, TILE), part), pl.BlockSpec((1, ROWS, TILE), part),
         whole((4, ROWS, TILE)), whole((4, ROWS, TILE)), HALO, HALO, whole((2, ROWS, TILE)), MSG,
         whole((ROWS, TILE))],
        whole((2 * ROWS, TILE)),
        sds((2 * ROWS, TILE)),
        [SQ, SQ, SQ, SQ],
    )(index, kh, vh, sig_k, evict, dst, dn, hk, hv, halo, got, gq)

    arrived = exchanged(grads.reshape(256, 1, 128), ALL).reshape(256, 128)
    copies = pl.pallas_call(total_kernel, out_shape=sds((256, 128)), name="total")(arrived)
    whole_sum = exchanged(copies.reshape(256, 1, 128), ALL).reshape(2, HEADS, RANK, DH)
    grad_q, grad_k = whole_sum.transpose(0, 1, 3, 2)
    return out, grad_q, grad_k


HALO_NAT = whole((TILE, HEADS, DH))


def solution(mesh):
    torus = Mesh(mesh.devices.reshape(8, 4, 2, mesh.shape["batch"]), ALL)
    rows = P("batch", SEQ, None, None)
    in_specs = (rows, rows, rows, P("batch", None, None), P(), P(), rows)
    return jax.shard_map(
        body, mesh=torus, in_specs=in_specs, out_specs=(rows, P(), P()), check_vma=False
    )
```

profile of v0, /device:TPU:1, one launch (start us, length us, event | category | flops | bytes accessed | tf_op | source)
XLA Modules:
  0.0 150.4 jit_solution(12692803501697140363)
XLA Ops:
  0.6 0.0 copy-start.5
  0.7 2.0 %slice_bitcast_fusion = bf16[128,16,128]{2,1,0:T(8,128)(2,1)} fusion(bf16[1,512,16,128]{3,2,1,0:T(8,128)(2,1)} %v_ref.1), kind=kLoop, calls=%fused_computation | loop fusion | bytes 1048576 | tf_op jit(solution)/shard_map/squeeze | solution.py:379
  2.7 4.6 %collective-permute-start.1 = (bf16[128,16,128]{2,1,0:T(8,128)(2,1)}, bf16[128,16,128]{2,1,0:T(8,128)(2,1)S(1)}, u32[]{:S(2)}, u32[]{:S(2)}) collective-permute-start(bf16[128,16,128]{2,1,0:T(8,128)(2,1)} %slice_bitcast_fusion), channel_id=1, source_target_pairs={{0,4},{4,8},{8,12},{12,16},{16,20},{20,24},{24,28},{28,32},{32,36}... | collective-permute-start | bytes 1572872 | tf_op jit(solution)/shard_map/ppermute | solution.py:379
  7.2 1.9 %slice_bitcast_fusion.1 = bf16[128,16,128]{2,1,0:T(8,128)(2,1)} fusion(bf16[1,512,16,128]{3,2,1,0:T(8,128)(2,1)} %k_ref.1), kind=kLoop, calls=%fused_computation.1 | loop fusion | bytes 1048576 | tf_op jit(solution)/shard_map/squeeze | solution.py:378
  9.1 1.9 %collective-permute-start = (bf16[128,16,128]{2,1,0:T(8,128)(2,1)}, bf16[128,16,128]{2,1,0:T(8,128)(2,1)S(1)}, u32[]{:S(2)}, u32[]{:S(2)}) collective-permute-start(bf16[128,16,128]{2,1,0:T(8,128)(2,1)} %slice_bitcast_fusion.1), channel_id=1, source_target_pairs={{0,4},{4,8},{8,12},{12,16},{16,20},{20,24},{24,28},{28,32},{32,36}... | collective-permute-start | bytes 1572872 | tf_op jit(solution)/shard_map/ppermute | solution.py:378
  11.1 0.0 copy-start.6
  11.1 1.6 %copy-done.6 = bf16[1,512,16,128]{3,2,1,0:T(8,128)(2,1)S(1)} copy-done((bf16[1,512,16,128]{3,2,1,0:T(8,128)(2,1)S(1)}, bf16[1,512,16,128]{3,2,1,0:T(8,128)(2,1)}, u32[]{:S(2)}) %copy-start.6) | copy-done | bytes 2097176
  12.7 0.7 copy-done.10
  13.4 5.5 %keys.1 = (bf16[16,512,128]{2,1,0:T(8,128)(2,1)S(1)}, bf16[16,512,128]{2,1,0:T(8,128)(2,1)S(1)}, f32[4,128,128]{2,1,0:T(8,128)S(1)}, f32[4,128,128]{2,1,0:T(8,12...) custom-call(s32[1]{0:T(128)} %bitcast.idx_ref, s32[16,256]{1,0:T(8,128)S(1)} %bitcast.25, ...), custom_call_target="tpu_custom_call" | custom-call | tf_op jit(solution)/shard_map/keys/pallas_call | solution.py:385
  18.9 1.3 copy-done
  20.2 1.3 copy-done.2
  21.6 22.7 %all_to_all.25.got_ref = f32[64,4,128]{2,1,0:T(4,128)S(1)} all-to-all(f32[64,4,128]{2,1,0:T(4,128)S(1)} %get-tuple-element.26), channel_id=1, replica_groups=mesh['z'=8,'y'=4,'core'=2,'batch'=4] {'z','y','core'}, dimensions={0} | all-to-all | bytes 262144 | tf_op jit(solution)/shard_map/all_to_all | solution.py:357
  44.3 0.0 collective-permute-done.1.hv_ref
  44.3 0.0 collective-permute-done.hk_ref
  44.3 25.7 %attend.1 = (bf16[16,512,128]{2,1,0:T(8,128)(2,1)S(1)}, bf16[16,512,128]{2,1,0:T(8,128)(2,1)S(1)}, f32[16,512,128]{2,1,0:T(8,128)}, f32[4,6,128,128]{3,2,1,0:T(8...) custom-call(s32[1]{0:T(128)} %bitcast.idx_ref, ...), custom_call_target="tpu_custom_call" | custom-call | tf_op jit(solution)/shard_map/attend/pallas_call | solution.py:395
  70.0 14.9 %all_to_all.26.got_ref = f32[64,4,128]{2,1,0:T(4,128)S(1)} all-to-all(f32[64,4,128]{2,1,0:T(4,128)S(1)} %get-tuple-element.33), channel_id=1, replica_groups=mesh['z'=8,'y'=4,'core'=2,'batch'=4] {'z','y','core'}, dimensions={0} | all-to-all | bytes 262144 | tf_op jit(solution)/shard_map/all_to_all | solution.py:357
  84.9 2.2 %copy-done.4 = f32[16,512,128]{2,1,0:T(8,128)S(1)} copy-done((f32[16,512,128]{2,1,0:T(8,128)S(1)}, f32[16,512,128]{2,1,0:T(8,128)}, u32[]{:S(2)}) %copy-start.4) | copy-done | bytes 4194328
  87.1 5.0 %output.1 = (bf16[1,512,16,128]{3,2,1,0:T(8,128)(2,1)}, f32[128,128]{1,0:T(8,128)S(1)}, f32[4,128,128]{2,1,0:T(8,128)S(1)}, f32[64,4,128]{2,1,0:T(4,128)S(1)}) custom-call(f32[16,512,128]{2,1,0:T(8,128)S(1)} %copy-done.4, bf16[16,512,128]{2,1,0:T(8,128)(2,1)S(1)} %get-tuple-element.28.qh_ref, bf16[16,512,128]{2,1,0:T(8,128)(2,1)S(1)} %get-tuple-element.29.ch_ref, ...), custom_call_target="tpu_custom_call" | custom-call | tf_op jit(solution)/shard_map/output/pallas_call | solution.py:407
  92.1 14.9 %all_to_all.27.got_ref = f32[64,4,128]{2,1,0:T(4,128)S(1)} all-to-all(f32[64,4,128]{2,1,0:T(4,128)S(1)} %get-tuple-element.41), channel_id=1, replica_groups=mesh['z'=8,'y'=4,'core'=2,'batch'=4] {'z','y','core'}, dimensions={0} | all-to-all | bytes 262144 | tf_op jit(solution)/shard_map/all_to_all | solution.py:357
  107.0 3.0 %key_grad.1 = f32[256,128]{1,0:T(8,128)S(1)} custom-call(s32[1]{0:T(128)} %bitcast.idx_ref, bf16[16,512,128]{2,1,0:T(8,128)(2,1)S(1)} %copy-done.1, bf16[16,512,128]{2,1,0:T(8,128)(2,1)S(1)} %copy-done.3, f32[4,128,128]{2,1,0:T(8,128)S(1)} %get-tuple-element.35.sig_ref, f32[4,128,128]{2,1,0:T(8,128)S(1)} %get-tuple-element.36.evict_ref, ...), custom_call_target="tpu_custom_call" | custom-call | tf_op jit(solution)/shard_map/key_grad/pallas_call | solution.py:419
  110.0 19.3 %all_to_all.28 = f32[256,1,128]{2,1,0:T(1,128)} all-to-all(f32[256,1,128]{2,1,0:T(1,128)S(1)} %bitcast.22), channel_id=1, replica_groups=mesh['z'=8,'y'=4,'core'=2,'batch'=4] {'z','y','core','batch'}, dimensions={0} | all-to-all | bytes 262144 | tf_op jit(solution)/shard_map/all_to_all | solution.py:357
  129.4 1.6 %total.1 = f32[256,128]{1,0:T(8,128)} custom-call(f32[256,128]{1,0:T(8,128)} %bitcast.29), custom_call_target="tpu_custom_call" | custom-call | tf_op jit(solution)/shard_map/total/pallas_call | solution.py:431
  131.0 18.8 %all_to_all.29 = f32[256,1,128]{2,1,0:T(1,128)S(1)} all-to-all(f32[256,1,128]{2,1,0:T(1,128)} %bitcast.30), channel_id=1, replica_groups=mesh['z'=8,'y'=4,'core'=2,'batch'=4] {'z','y','core','batch'}, dimensions={0} | all-to-all | bytes 262144 | tf_op jit(solution)/shard_map/all_to_all | solution.py:357
  149.7 0.7 slice_bitcast_fusion.2
  (17 shorter events, 0.0 us)
Async XLA Ops:
  0.6 10.4 %copy-start.5 = (bf16[1,512,16,128]{3,2,1,0:T(8,128)(2,1)S(1)}, bf16[1,512,16,128]{3,2,1,0:T(8,128)(2,1)}, u32[]{:S(2)}) copy-start(bf16[1,512,16,128]{3,2,1,0:T(8,128)(2,1)} %k_ref.1) | copy-start | bytes 6291460
  0.6 10.4 %copy-start.9 = (bf16[16,128,8]{1,2,0:T(8,128)(2,1)S(1)}, bf16[16,128,8]{1,2,0:T(8,128)(2,1)}, u32[]{:S(2)}) copy-start(bf16[16,128,8]{1,2,0:T(8,128)(2,1)} %param.12) | copy-start | bytes 98308
  2.7 41.6 %collective-permute-start.1 = (bf16[128,16,128]{2,1,0:T(8,128)(2,1)}, bf16[128,16,128]{2,1,0:T(8,128)(2,1)S(1)}, u32[]{:S(2)}, u32[]{:S(2)}) collective-permute-start(bf16[128,16,128]{2,1,0:T(8,128)(2,1)} %slice_bitcast_fusion), channel_id=1, source_target_pairs={{0,4},{4,8},{8,12},{12,16},{16,20},{20,24},{24,28},{28,32},{32,36}... | collective-permute-start | bytes 1572872 | tf_op jit(solution)/shard_map/ppermute | solution.py:379
  9.1 35.2 %collective-permute-start = (bf16[128,16,128]{2,1,0:T(8,128)(2,1)}, bf16[128,16,128]{2,1,0:T(8,128)(2,1)S(1)}, u32[]{:S(2)}, u32[]{:S(2)}) collective-permute-start(bf16[128,16,128]{2,1,0:T(8,128)(2,1)} %slice_bitcast_fusion.1), channel_id=1, source_target_pairs={{0,4},{4,8},{8,12},{12,16},{16,20},{20,24},{24,28},{28,32},{32,36}... | collective-permute-start | bytes 1572872 | tf_op jit(solution)/shard_map/ppermute | solution.py:378
  11.1 1.6 %copy-start.6 = (bf16[1,512,16,128]{3,2,1,0:T(8,128)(2,1)S(1)}, bf16[1,512,16,128]{3,2,1,0:T(8,128)(2,1)}, u32[]{:S(2)}) copy-start(bf16[1,512,16,128]{3,2,1,0:T(8,128)(2,1)} %v_ref.1) | copy-start | bytes 6291460
  12.7 0.7 copy-start.10
  13.4 30.9 %copy-start.7 = (bf16[1,512,16,128]{3,2,1,0:T(8,128)(2,1)S(1)}, bf16[1,512,16,128]{3,2,1,0:T(8,128)(2,1)}, u32[]{:S(2)}) copy-start(bf16[1,512,16,128]{3,2,1,0:T(8,128)(2,1)} %q_ref.1) | copy-start | bytes 6291460
  13.4 30.9 %copy-start.8 = (bf16[1,512,16,128]{3,2,1,0:T(8,128)(2,1)S(1)}, bf16[1,512,16,128]{3,2,1,0:T(8,128)(2,1)}, u32[]{:S(2)}) copy-start(bf16[1,512,16,128]{3,2,1,0:T(8,128)(2,1)} %c_ref.1) | copy-start | bytes 6291460
  13.4 31.0 %copy-start.11 = (bf16[16,128,8]{1,2,0:T(8,128)(2,1)S(1)}, bf16[16,128,8]{1,2,0:T(8,128)(2,1)}, u32[]{:S(2)}) copy-start(bf16[16,128,8]{1,2,0:T(8,128)(2,1)} %param.11) | copy-start | bytes 98308
  18.9 1.4 copy-start
  20.2 1.4 copy-start.2
  84.9 2.2 %copy-start.4 = (f32[16,512,128]{2,1,0:T(8,128)S(1)}, f32[16,512,128]{2,1,0:T(8,128)}, u32[]{:S(2)}) copy-start(f32[16,512,128]{2,1,0:T(8,128)} %get-tuple-element.27.numer_ref) | copy-start | bytes 12582916
  87.1 19.9 %copy-start.1 = (bf16[16,512,128]{2,1,0:T(8,128)(2,1)S(1)}, bf16[16,512,128]{2,1,0:T(8,128)(2,1)}, u32[]{:S(2)}) copy-start(bf16[16,512,128]{2,1,0:T(8,128)(2,1)} %copy-done) | copy-start | bytes 6291460
  87.1 19.9 %copy-start.3 = (bf16[16,512,128]{2,1,0:T(8,128)(2,1)S(1)}, bf16[16,512,128]{2,1,0:T(8,128)(2,1)}, u32[]{:S(2)}) copy-start(bf16[16,512,128]{2,1,0:T(8,128)(2,1)} %copy-done.2) | copy-start | bytes 6291460
where the time goes:
time: 151 us; the launch traced here: 150 us
  blocking collectives  90.6 us (60%)
  Pallas kernels  40.8 us (27%)
  local copies, waits for them, and re-layouts  11.8 us (8%)
  starting transfers between devices  6.48 us (4%)
    all_to_all x5, blocking collectives, exchanged(): return lax.all_to_all(x, axes, split_axis=0, concat_axis=0, tiled=True)  90.6 us
    pallas_call x1, Pallas kernels, body(): call(attend_kernel, 'attend', 4, [SMEM, SMEM, NAT, NAT, BYHEAD, BYHEAD, H...  25.7 us
    unnamed x24, local copies, waits for them, and re-layouts  7.21 us
    pallas_call x1, Pallas kernels, body(): call(keys_kernel, 'keys', 4, [SMEM, SMEM, NAT, NAT, MAPS], [BYHEAD, BYHEA...  5.48 us
    pallas_call x1, Pallas kernels, body(): call(output_kernel, 'output', 4, [BYHEAD, BYHEAD, BYHEAD, STATS, PREV, wh...  5.01 us
    ppermute x1, starting transfers between devices, body(): halo_v = lax.ppermute(values[0, 3 * TILE:], SEQ, steps)  4.57 us
  transfers between devices with their start and end apart: 2, of which 0 were waited for; matrix products, arithmetic and copies ran while one was open for 1% of the time, Pallas kernels for 4%

commit v1 on v0

v1 whole, which is shorter than its diff:
```python
import math

import jax
import jax.numpy as jnp
from jax import lax
from jax.experimental import pallas as pl
from jax.experimental.pallas import tpu as pltpu
from jax.sharding import Mesh
from jax.sharding import PartitionSpec as P

TILE = 128
HEADS = 16
RANK = 8
DH = 128
ROWS = HEADS * RANK
SEQ = ("z", "y", "core")
ALL = ("z", "y", "core", "batch")
SHIFT = 1.5
SCALE = 1.0 / math.sqrt(DH)
SCALE_LOG2 = SCALE * math.log2(math.e)
NEG = -1e30
VMEM = 67_043_328
F32 = jnp.float32
BF16 = jnp.bfloat16
NN = (((1,), (0,)), ((), ()))
NT = (((1,), (1,)), ((), ()))
TN = (((0,), (0,)), ((), ()))


def dot(a, b, dims=NN):
    return lax.dot_general(a, b, dims, preferred_element_type=F32)


def halves(x):
    hi = x.astype(BF16)
    return hi, (x - hi.astype(F32)).astype(BF16)


def stacked(*parts):
    rows = []
    for x in parts:
        hi = x.astype(BF16).astype(F32)
        rows += [hi, x - hi]
    return jnp.concatenate(rows, 0).astype(BF16)


def folded(x, at=0):
    return x[at : at + RANK] + x[at + RANK : at + 2 * RANK]


def row_sums(x):
    ones = jnp.ones((8, 128), BF16)
    hi, lo = halves(x)
    return dot(ones, hi, NT) + dot(ones, lo, NT)


def softplus_sigmoid(pre):
    e = jnp.exp(-jnp.abs(pre))
    value = jnp.maximum(pre, 0.0) + jnp.log1p(e)
    inv = 1.0 / (1.0 + e)
    return value, jnp.where(pre >= 0, inv, e * inv)


def per_head_sum(x):
    x = x.reshape(HEADS, RANK, TILE)
    x = jnp.broadcast_to(jnp.sum(x, 1, keepdims=True), x.shape)
    return x.reshape(ROWS, TILE)


def of(h):
    return pl.ds(h * RANK, RANK)


def lane_sums(x):
    return jnp.broadcast_to(jnp.sum(x, 1, keepdims=True), (ROWS, TILE))


def keys_kernel(idx_ref, cnt_ref, k_ref, v_ref, kmap_ref, kh_ref, vh_ref, halo_ref, local_ref,
                sig_ref, evict_ref, nloc_ref, msg_ref, pre, evict, st_all, st_ev, all_acc, nacc,
                feats, msg):
    n = pl.program_id(0)

    @pl.when(n == 0)
    def _():
        all_acc[...] = jnp.zeros_like(all_acc)
        nacc[...] = jnp.zeros_like(nacc)

    kh_ref[...] = jnp.swapaxes(k_ref[0], 0, 1)
    vh_ref[...] = jnp.swapaxes(v_ref[0], 0, 1)
    lanes = lax.broadcasted_iota(jnp.int32, (RANK, TILE), 1)
    for h in range(HEADS):
        pre[of(h), :] = dot(kmap_ref[h], kh_ref[h], NT)
        count = cnt_ref[h, idx_ref[0] * 4 + n]
        evict[of(h), :] = (lanes >= count).astype(F32)
    feat, sig = softplus_sigmoid(pre[...] - SHIFT)
    ev = feat * evict[...]
    feats[0] = feat
    feats[1] = ev
    for h in range(HEADS):
        res = dot(stacked(feats[0, of(h), :], feats[1, of(h), :]), vh_ref[h])
        st_all[of(h), :] = folded(res)
        st_ev[of(h), :] = folded(res, 2 * RANK)
    evict_ref[0] = evict[...]
    sig_ref[0] = sig
    local_ref[0] = all_acc[...] + st_ev[...]
    all_acc[...] += st_all[...]
    nloc_ref[0] = lane_sums(ev) + nacc[...]
    nacc[...] += lane_sums(feat)

    @pl.when(n == 3)
    def _():
        halo_ref[0] = kh_ref[...]
        halo_ref[1] = vh_ref[...]
        row = row_sums(nacc[...] * (1.0 / 128.0))
        for s in range(64):
            msg[s, 0:2, :] = all_acc[2 * s : 2 * s + 2, :]
            msg[s, 2:4, :] = row[0:2]
        msg_ref[...] = msg[...]


def attention(kp_ref, ko_ref, vp_ref, vo_ref, qmap_ref, count_of, qs, cs, raw_ref, numer_ref,
              scores, weights, vv, pre, mx, den, cn):
    zeros = jnp.zeros((RANK, DH), F32)
    for h in range(HEADS):
        vv[h, 0:TILE, :] = vp_ref[h]
        vv[h, TILE:, :] = vo_ref[h]
        top = jnp.concatenate([qmap_ref[h].astype(F32), zeros], 0).astype(BF16)
        res = dot(jnp.concatenate([top, kp_ref[h], ko_ref[h]], 0), qs[h], NT)
        pre[of(h), :] = res[:RANK]
        scores[h] = res[2 * RANK :]
    rows = lax.broadcasted_iota(jnp.int32, (TILE, TILE), 0)
    cols = lax.broadcasted_iota(jnp.int32, (TILE, TILE), 1)
    causal = rows <= cols
    for h in range(HEADS):
        s_prev = jnp.where(rows < count_of(h), scores[h, 0:TILE, :], NEG)
        s_own = jnp.where(causal, scores[h, TILE:, :], NEG)
        top = jnp.max(jnp.maximum(s_prev, s_own), 0, keepdims=True)
        w_prev = jnp.exp2((s_prev - top) * SCALE_LOG2)
        w_own = jnp.exp2((s_own - top) * SCALE_LOG2)
        weights[h, 0:TILE, :] = w_prev.astype(BF16)
        weights[h, TILE:, :] = w_own.astype(BF16)
        sums = jnp.sum(w_prev + w_own, 0, keepdims=True)
        mx[of(h), :] = jnp.broadcast_to(top, (RANK, TILE))
        den[of(h), :] = jnp.broadcast_to(sums, (RANK, TILE))
    for h in range(HEADS):
        w = weights[h]
        against = w.astype(F32) * dot(vv[h], cs[h], NT)
        cn[of(h), :] = jnp.broadcast_to(jnp.sum(against, 0, keepdims=True), (RANK, TILE))
        numer_ref[h] = dot(w, vv[h], TN)
    feat, sig = softplus_sigmoid(pre[...] - SHIFT)
    raw_ref[0, 0] = feat
    raw_ref[0, 1] = sig
    raw_ref[0, 2] = jnp.exp(-(mx[...] * SCALE))
    raw_ref[0, 3] = den[...]
    raw_ref[0, 4] = cn[...]


def near_kernel(idx_ref, cnt_ref, q_ref, c_ref, kp_ref, ko_ref, vp_ref, vo_ref, qmap_ref, qh_ref,
                ch_ref, numer_ref, raw_ref, qs, cs, *scratch):
    t = pl.program_id(0)
    qs[...] = jnp.swapaxes(q_ref[0], 0, 1)
    cs[...] = jnp.swapaxes(c_ref[0], 0, 1)

    @pl.when(t > 0)
    def _():
        before = idx_ref[0] * 4 + jnp.maximum(t - 1, 0)
        attention(kp_ref, ko_ref, vp_ref, vo_ref, qmap_ref, lambda h: cnt_ref[h, before], qs, cs,
                  raw_ref, numer_ref, *scratch)

    qh_ref[...] = qs[...]
    ch_ref[...] = cs[...]


def first_kernel(idx_ref, cnt_ref, qh_ref, ch_ref, halo_in, ko_ref, vo_ref, qmap_ref, kmap_ref,
                 numer_any, raw_any, numer_ref, raw_ref, halo_ref, nhalo_ref, qs, cs, kept, feats,
                 *scratch):
    del numer_any, raw_any
    index = idx_ref[0]
    before = jnp.maximum(index * 4 - 1, 0)
    pre = scratch[3]
    lanes = lax.broadcasted_iota(jnp.int32, (RANK, TILE), 1)
    counts = [jnp.where(index > 0, cnt_ref[h, before], 0) for h in range(HEADS)]
    qs[...] = qh_ref[...]
    cs[...] = ch_ref[...]
    for h in range(HEADS):
        pre[of(h), :] = dot(kmap_ref[h], halo_in[0, h], NT)
        kept[of(h), :] = (lanes < counts[h]).astype(F32)
    feat, sig = softplus_sigmoid(pre[...] - SHIFT)
    feat = feat * kept[...]
    feats[...] = feat
    for h in range(HEADS):
        feats[of(h), :] = folded(dot(stacked(feats[of(h), :]), halo_in[1, h]))
    halo_ref[0] = feats[...]
    halo_ref[1] = kept[...] * sig
    nhalo_ref[...] = lane_sums(feat)
    attention(halo_in.at[0], ko_ref, halo_in.at[1], vo_ref, qmap_ref, lambda h: counts[h], qs, cs,
              raw_ref, numer_ref, *scratch)


def total_kernel(idx_ref, raw_ref, ch_ref, nloc_ref, nhalo_ref, got_ref, st_ref, dst_ref, msg_ref,
                 norm, norm_t, cf, dst, dacc, msg):
    t = pl.program_id(0)
    index = idx_ref[0]

    @pl.when(t == 0)
    def _():
        dacc[...] = jnp.zeros_like(dacc)
        run = jnp.zeros((2, 128), F32)
        nrun = jnp.zeros((1, 128), F32)
        for s in range(64):
            msg[s, 0:2, :] = run
            run = run + got_ref[s, 0:2, :]
            nrun = nrun + jnp.where(s < index, got_ref[s, 2:3, :], 0.0)
        norm[...] = jnp.broadcast_to(nrun, (128, 128)).T
        norm_t[...] = norm[...] - nhalo_ref[...]

    @pl.when(t > 0)
    def _():
        norm_t[...] = norm[...] + nloc_ref[0]

    feat = raw_ref[0, 0]
    decay = raw_ref[0, 2]
    rinv = 1.0 / (raw_ref[0, 3] + decay * per_head_sum(feat * norm_t[...]))
    coef = decay * rinv
    cf[...] = feat * coef
    for h in range(HEADS):
        dst[of(h), :] = folded(dot(stacked(cf[of(h), :]), ch_ref[h]))
    st_ref[0, 0] = coef
    st_ref[0, 1] = rinv
    st_ref[0, 2] = norm_t[...]
    dst_ref[0] = dst[...]
    dacc[...] += dst[...]

    @pl.when(t == 3)
    def _():
        for s in range(64):
            msg[s, 2:4, :] = dacc[2 * s : 2 * s + 2, :]
        msg_ref[...] = msg[...]


def state_kernel(raw_ref, st_ref, ch_ref, local_ref, halo_ref, got_ref, state_ref, pre_ref, dn_ref,
                 msg_ref, far, state, grad, drow, msg):
    t = pl.program_id(0)

    @pl.when(t == 0)
    def _():
        drow[...] = jnp.zeros_like(drow)
        run = jnp.zeros((2, 128), F32)
        for s in reversed(range(64)):
            far[2 * s : 2 * s + 2, :] = got_ref[s, 0:2, :]
            msg[s, 0:2, :] = run
            run = run + got_ref[s, 2:4, :]
        state[...] = far[...] - halo_ref[0]

    @pl.when(t > 0)
    def _():
        state[...] = far[...] + local_ref[0]

    for h in range(HEADS):
        grad[of(h), :] = folded(dot(stacked(state[of(h), :]), ch_ref[h], NT))
    state_ref[0] = state[...]
    coef = st_ref[0, 0]
    cf = raw_ref[0, 0] * coef
    along = raw_ref[0, 4] * st_ref[0, 1] + per_head_sum(cf * grad[...])
    pre_ref[0] = coef * (grad[...] - along * st_ref[0, 2]) * raw_ref[0, 1]
    dn = -(cf * along)
    dn_ref[0] = lane_sums(dn)
    drow[...] += row_sums(dn)

    @pl.when(t == 3)
    def _():
        for s in range(64):
            msg[s, 2:4, :] = drow[0:2, :]
        msg_ref[...] = msg[...]


def output_kernel(numer_ref, raw_ref, st_ref, state_ref, pre_ref, qh_ref, out_ref, gq_ref, cf,
                  rinv, state, pre, out, gq):
    t = pl.program_id(0)

    @pl.when(t == 0)
    def _():
        gq[...] = jnp.zeros_like(gq)

    cf[...] = raw_ref[0, 0] * st_ref[0, 0]
    rinv[...] = st_ref[0, 1]
    state[...] = state_ref[0]
    pre[...] = pre_ref[0]
    sub = lax.broadcasted_iota(jnp.int32, (RANK, TILE), 0)
    ones = jnp.ones((RANK, DH), F32)
    zeros = jnp.zeros((RANK, DH), F32)
    for h in range(HEADS):
        s = state[of(h), :]
        s_hi = s.astype(BF16).astype(F32)
        s_lo = s - s_hi
        c = cf[of(h), :]
        c_hi = c.astype(BF16).astype(F32)
        r = rinv[of(h), :]
        r_hi = r.astype(BF16).astype(F32)
        r_mid = (r - r_hi).astype(BF16).astype(F32)
        pieces = jnp.where(sub == 0, r_hi, jnp.where(sub == 1, r_mid, r - r_hi - r_mid))
        pieces = jnp.where(sub < 3, pieces, 0.0)
        lhs = jnp.concatenate([c_hi, c - c_hi, c_hi, pieces], 0).astype(BF16)
        left = jnp.concatenate([s_hi, s_hi, s_lo, zeros], 0)
        right = jnp.concatenate([zeros, zeros, zeros, ones], 0)
        both = dot(lhs, jnp.concatenate([left, right], 1).astype(BF16), TN)
        out[h] = (numer_ref[h] * both[:, DH:] + both[:, :DH]).astype(BF16)
        gq[of(h), :] += folded(dot(stacked(pre[of(h), :]), qh_ref[h]))
    out_ref[0] = jnp.swapaxes(out[...], 0, 1)

    @pl.when(t == 3)
    def _():
        gq_ref[...] = gq[...]


def key_grad_kernel(idx_ref, kh_ref, vh_ref, sig_ref, evict_ref, dst_ref, dn_ref, halo_in,
                    halo_ref, got_ref, gq_ref, out_ref, acc, nacc, grad, ev, near, gk):
    i = pl.program_id(0)
    n = 3 - i
    index = idx_ref[0]

    @pl.when(i == 0)
    def _():
        nrun = jnp.zeros((1, 128), F32)
        for s in range(64):
            acc[2 * s : 2 * s + 2, :] = got_ref[s, 0:2, :]
            nrun = nrun + jnp.where(s > index, got_ref[s, 2:3, :], 0.0)
        nacc[...] = jnp.broadcast_to(nrun, (128, 128)).T
        near[...] = dst_ref[0]
        for h in range(HEADS):
            grad[of(h), :] = folded(dot(stacked(near[of(h), :]), halo_in[1, h], NT))
        grad[...] = -(grad[...] + dn_ref[0]) * halo_ref[1]
        for h in range(HEADS):
            gk[of(h), :] = folded(dot(stacked(grad[of(h), :]), halo_in[0, h]))

    @pl.when(i >= 2)
    def _():
        acc[...] += dst_ref[jnp.minimum(n + 2, 3)]
        nacc[...] += dn_ref[jnp.minimum(n + 2, 3)]

    after = jnp.minimum(n + 1, 3)
    live = (n < 3).astype(F32)
    near[...] = dst_ref[after] * live
    for h in range(HEADS):
        res = dot(stacked(acc[of(h), :], near[of(h), :]), vh_ref[h], NT)
        grad[of(h), :] = folded(res)
        ev[of(h), :] = folded(res, 2 * RANK)
    grad[...] = (
        grad[...] + nacc[...] + evict_ref[0] * (ev[...] + dn_ref[after] * live)
    ) * sig_ref[0]
    for h in range(HEADS):
        gk[of(h), :] += folded(dot(stacked(grad[of(h), :]), kh_ref[h]))

    @pl.when(i == 3)
    def _():
        out_ref[:ROWS, :] = gq_ref[...]
        out_ref[ROWS:, :] = gk[...]


def spread_kernel(x_ref, o_ref):
    o_ref[...] = jnp.broadcast_to(jnp.sum(x_ref[...], 0, keepdims=True), o_ref.shape)


def sds(shape, dtype=F32):
    return jax.ShapeDtypeStruct(shape, dtype)


def whole(*shape):
    return pl.BlockSpec(shape, lambda *_: (0,) * len(shape))


def by_head(index):
    return pl.BlockSpec((HEADS, TILE, DH), lambda t: (0, index(t), 0))


def part(index, *lead):
    zeros = (0,) * (len(lead) + 2)
    return pl.BlockSpec((1, *lead, ROWS, TILE), lambda t: (index(t), *zeros))


def same(t):
    return t


def first(t):
    return 0


def prev(t):
    return jnp.maximum(t - 1, 0)


def back(t):
    return 3 - t


SMEM = pl.BlockSpec(memory_space=pltpu.SMEM)
ANY = pl.BlockSpec(memory_space=pl.ANY)
MAPS = whole(HEADS, RANK, DH)
MSG = whole(64, 4, 128)
MSG_T = sds((64, 4, 128))
MSG_S = pltpu.VMEM((64, 4, 128), F32)
NAT = pl.BlockSpec((1, TILE, HEADS, DH), lambda t: (0, t, 0, 0))
HALO = whole(2, HEADS, TILE, DH)
PAIR = whole(2, ROWS, TILE)
BIG = sds((HEADS, 4 * TILE, DH), BF16)
PARTS = sds((4, ROWS, TILE))
SQ = pltpu.VMEM((ROWS, TILE), F32)
HEAD_S = pltpu.VMEM((HEADS, TILE, DH), BF16)
ATTEND_S = [
    pltpu.VMEM((HEADS, 2 * TILE, TILE), F32),
    pltpu.VMEM((HEADS, 2 * TILE, TILE), BF16),
    pltpu.VMEM((HEADS, 2 * TILE, DH), BF16),
    SQ, SQ, SQ, SQ,
]


def exchanged(x, axes):
    return lax.all_to_all(x, axes, split_axis=0, concat_axis=0, tiled=True)


def call(kernel, name, grid, in_specs, out_specs, out_shape, scratch, us, aliases=None):
    return pl.pallas_call(
        kernel,
        grid=(grid,),
        in_specs=in_specs,
        out_specs=out_specs,
        out_shape=out_shape,
        scratch_shapes=scratch,
        name=name,
        input_output_aliases=aliases or {},
        cost_estimate=pl.CostEstimate(
            flops=int(us * 2e8), bytes_accessed=int(us * 1e6), transcendentals=0
        ),
        compiler_params=pltpu.CompilerParams(
            dimension_semantics=("arbitrary",), vmem_limit_bytes=VMEM
        ),
    )


def body(queries, keys, values, keep_count, query_map, key_map, cotangent):
    count = lax.axis_size(SEQ)
    steps = [(i, i + 1) for i in range(count - 1)]
    index = lax.axis_index(SEQ).astype(jnp.int32).reshape(1)
    counts = keep_count[0]
    qmap = query_map.transpose(0, 2, 1)
    kmap = key_map.transpose(0, 2, 1)

    kh, vh, edge, local, sig_k, evict, nloc, msg = call(
        keys_kernel, "keys", 4,
        [SMEM, SMEM, NAT, NAT, MAPS],
        [by_head(same), by_head(same), HALO, part(same), part(same), part(same), part(same), MSG],
        [BIG, BIG, sds((2, HEADS, TILE, DH), BF16), PARTS, PARTS, PARTS, PARTS, MSG_T],
        [SQ, SQ, SQ, SQ, SQ, SQ, pltpu.VMEM((2, ROWS, TILE), F32), MSG_S],
        4,
    )(index, counts, keys, values, kmap)

    halo_kv = lax.ppermute(edge, SEQ, steps)
    got = exchanged(msg, SEQ)

    qh, ch, numer, raw = call(
        near_kernel, "near", 4,
        [SMEM, SMEM, NAT, NAT, by_head(prev), by_head(same), by_head(prev), by_head(same), MAPS],
        [by_head(same), by_head(same), by_head(same), part(same, 5)],
        [BIG, BIG, sds((HEADS, 4 * TILE, DH)), sds((4, 5, ROWS, TILE))],
        [HEAD_S, HEAD_S, *ATTEND_S],
        8,
    )(index, counts, queries, cotangent, kh, kh, vh, vh, qmap)

    numer, raw, halo, nhalo = call(
        first_kernel, "first", 1,
        [SMEM, SMEM, by_head(first), by_head(first), HALO, by_head(first), by_head(first), MAPS,
         MAPS, ANY, ANY],
        [by_head(first), part(first, 5), PAIR, whole(ROWS, TILE)],
        [sds((HEADS, 4 * TILE, DH)), sds((4, 5, ROWS, TILE)), sds((2, ROWS, TILE)),
         sds((ROWS, TILE))],
        [HEAD_S, HEAD_S, SQ, SQ, *ATTEND_S],
        3,
        {9: 0, 10: 1},
    )(index, counts, qh, ch, halo_kv, kh, vh, qmap, kmap, numer, raw)

    st, dst, msg = call(
        total_kernel, "total", 4,
        [SMEM, part(same, 5), by_head(same), part(prev), whole(ROWS, TILE), MSG],
        [part(same, 3), part(same), MSG],
        [sds((4, 3, ROWS, TILE)), PARTS, MSG_T],
        [SQ, SQ, SQ, SQ, SQ, MSG_S],
        2,
    )(index, raw, ch, nloc, nhalo, got)

    got = exchanged(msg, SEQ)

    state, pre_q, dn, msg = call(
        state_kernel, "state", 4,
        [part(same, 5), part(same, 3), by_head(same), part(prev), PAIR, MSG],
        [part(same), part(same), part(same), MSG],
        [PARTS, PARTS, PARTS, MSG_T],
        [SQ, SQ, SQ, pltpu.VMEM((8, 128), F32), MSG_S],
        2,
    )(raw, st, ch, local, halo, got)

    got = exchanged(msg, SEQ)

    out, gq = call(
        output_kernel, "output", 4,
        [by_head(same), part(same, 5), part(same, 3), part(same), part(same), by_head(same)],
        [NAT, whole(ROWS, TILE)],
        [sds((1, 4 * TILE, HEADS, DH), BF16), sds((ROWS, TILE))],
        [SQ, SQ, SQ, SQ, HEAD_S, SQ],
        4,
    )(numer, raw, st, state, pre_q, qh)

    grads = call(
        key_grad_kernel, "key_grad", 4,
        [SMEM, by_head(back), by_head(back), part(back), part(back), whole(4, ROWS, TILE),
         whole(4, ROWS, TILE), HALO, PAIR, MSG, whole(ROWS, TILE)],
        whole(2 * ROWS, TILE),
        sds((2 * ROWS, TILE)),
        [SQ, SQ, SQ, SQ, SQ, SQ],
        3,
    )(index, kh, vh, sig_k, evict, dst, dn, halo_kv, halo, got, gq)

    spread = call(
        spread_kernel, "spread", 1, [whole(16, 16, 128)], whole(16, 16, 128), sds((16, 16, 128)),
        [], 1,
    )
    grads = exchanged(grads.reshape(16, 16, 128), ("z", "core"))
    grads = exchanged(spread(grads), ("y", "batch"))
    grads = exchanged(spread(grads), ("z", "core"))
    grad_q, grad_k = grads.reshape(2, HEADS, RANK, DH).transpose(0, 1, 3, 2)
    return out, grad_q, grad_k


def solution(mesh):
    torus = Mesh(mesh.devices.reshape(8, 4, 2, mesh.shape["batch"]), ALL)
    rows = P("batch", SEQ, None, None)
    in_specs = (rows, rows, rows, P("batch", None, None), P(), P(), rows)
    return jax.shard_map(
        body, mesh=torus, in_specs=in_specs, out_specs=(rows, P(), P()), check_vma=False
    )
```

time: 151 us -> 137 us (0.907)
  blocking collectives: 90.6 us -> 60.6 us
  starting transfers between devices: 6.48 us -> 21.5 us
  local copies, waits for them, and re-layouts: 11.8 us -> 0.66 us
  Pallas kernels: 40.8 us -> 47.6 us
  waiting for transfers between devices: 0.01 us -> 4.73 us
    all_to_all x5 -> x4, blocking collectives: 90.6 us -> 60.6 us  [exchanged(): return lax.all_to_all(x, axes, split_axis=0, concat_axis=0, tiled=True)]
    all_to_all x0 -> x2, starting transfers between devices: none -> 16.9 us  [exchanged(): return lax.all_to_all(x, axes, split_axis=0, concat_axis=0, tiled=True)]
    unnamed x24 -> x0, local copies, waits for them, and re-layouts: 7.21 us -> none
    pallas_call x5 -> x9, Pallas kernels: 40.8 us -> 47.6 us  [the longest x1 10.5 us: body(): call(near_kernel, 'near', 4, [SMEM, SMEM, NAT, NAT, by_head(prev), by_hea...]
    all_to_all x0 -> x2, waiting for transfers between devices: none -> 4.73 us  [exchanged(): return lax.all_to_all(x, axes, split_axis=0, concat_axis=0, tiled=True)]
    squeeze x2 -> x0, local copies, waits for them, and re-layouts: 3.89 us -> none  [the longest x1 2.01 us: body(): halo_v = lax.ppermute(values[0, 3 * TILE:], SEQ, steps)]
    ppermute x2 -> x1, starting transfers between devices: 6.48 us -> 4.58 us  [body(): halo_kv = lax.ppermute(edge, SEQ, steps)]
  transfers between devices with their start and end apart: 2 -> 3, of which waited for: 0 -> 1; matrix products, arithmetic and copies ran while one was open for 1% -> 0% of each run, Pallas kernels for 4% -> 16%
where the time goes in v1:
time: 137 us; the launch traced here: 136 us
  blocking collectives  60.6 us (44%)
  Pallas kernels  47.6 us (35%)
  starting transfers between devices  21.5 us (16%)
  waiting for transfers between devices  4.73 us (3%)
    all_to_all x4, blocking collectives, exchanged(): return lax.all_to_all(x, axes, split_axis=0, concat_axis=0, tiled=True)  60.6 us
    all_to_all x2, starting transfers between devices, exchanged(): return lax.all_to_all(x, axes, split_axis=0, concat_axis=0, tiled=True)  16.9 us
    pallas_call x1, Pallas kernels, body(): call(near_kernel, 'near', 4, [SMEM, SMEM, NAT, NAT, by_head(prev), by_hea...  10.5 us
    pallas_call x1, Pallas kernels, body(): call(keys_kernel, 'keys', 4, [SMEM, SMEM, NAT, NAT, MAPS], [by_head(same)...  6.8 us
    pallas_call x1, Pallas kernels, body(): call(output_kernel, 'output', 4, [by_head(same), part(same, 5), part(same...  6.43 us
    pallas_call x1, Pallas kernels, body(): call(key_grad_kernel, 'key_grad', 4, [SMEM, by_head(back), by_head(back),...  5.94 us
    pallas_call x1, Pallas kernels, body(): call(state_kernel, 'state', 4, [part(same, 5), part(same, 3), by_head(sam...  5.19 us
    pallas_call x1, Pallas kernels, body(): call(first_kernel, 'first', 1, [SMEM, SMEM, by_head(first), by_head(first...  4.89 us
  transfers between devices with their start and end apart: 3, of which 1 were waited for; matrix products, arithmetic and copies ran while one was open for 0% of the time, Pallas kernels for 16%

profile of v1, /device:TPU:1, one launch (start us, length us, event | category | flops | bytes accessed | tf_op | source)
XLA Modules:
  0.0 135.8 jit_solution(13106053940431171418)
XLA Ops:
  0.6 6.8 %keys.1 = (bf16[16,512,128]{2,1,0:T(8,128)(2,1)}, bf16[16,512,128]{2,1,0:T(8,128)(2,1)}, bf16[2,16,128,128]{3,2,1,0:T(8,128)(2,1)}, f32[4,128,128]{2,1,0:T(8,128...) custom-call(s32[1]{0:T(128)} %bitcast.idx_ref, ...), custom_call_target="tpu_custom_call" | custom-call | flops 800000000 | bytes 4000000 | tf_op jit(solution)/shard_map/keys/pallas_call | solution.py:449
  7.4 4.6 %collective-permute-start = (bf16[2,16,128,128]{3,2,1,0:T(8,128)(2,1)}, bf16[2,16,128,128]{3,2,1,0:T(8,128)(2,1)}, u32[]{:S(2)}, u32[]{:S(2)}) collective-permute-start(bf16[2,16,128,128]{3,2,1,0:T(8,128)(2,1)} %get-tuple-element.32), channel_id=1, source_target_pairs={{0,4},{4,8},{8,12},{12,16},{16,20},{20,24},{24,28},{28,32},{32,36}... | collective-permute-start | bytes 3145736 | tf_op jit(solution)/shard_map/ppermute | solution.py:458
  12.0 11.7 %all-to-all-start = ((f32[64,4,128]{2,1,0:T(4,128)}), f32[64,4,128]{2,1,0:T(4,128)}, u32[]{:S(2)}, u32[]{:S(2)}) async-start(f32[64,4,128]{2,1,0:T(4,128)} %get-tuple-element.39), calls=%async_computation | async-start | bytes 262144 | tf_op jit(solution)/shard_map/all_to_all | solution.py:419
  23.7 10.5 %near.1 = (bf16[16,512,128]{2,1,0:T(8,128)(2,1)}, bf16[16,512,128]{2,1,0:T(8,128)(2,1)}, f32[16,512,128]{2,1,0:T(8,128)}, f32[4,5,128,128]{3,2,1,0:T(8,128)}) custom-call(s32[1]{0:T(128)} %bitcast.idx_ref, s32[16,256]{1,0:T(8,128)} %bitcast.15, bf16[1,512,16,128]{3,2,1,0:T(8,128)(2,1)} %q_ref.1, bf16[1,512,16,128]{3,2,1,0:T(8,128)(2,1)} %c_ref.1, ...), custom_call_target="tpu_custom_call" | custom-call | flops 1600000000 | bytes 8000000 | tf_op jit(solution)/shard_map/near/pallas_call | solution.py:461
  34.3 0.0 collective-permute-done.halo_in
  34.3 4.9 %first.1 = (f32[16,512,128]{2,1,0:T(8,128)}, f32[4,5,128,128]{3,2,1,0:T(8,128)}, f32[2,128,128]{2,1,0:T(8,128)}, f32[128,128]{1,0:T(8,128)}) custom-call(s32[1]{0:T(128)} %bitcast.idx_ref, s32[16,256]{1,0:T(8,128)} %bitcast.16, bf16[16,512,128]{2,1,0:T(8,128)(2,1)} %get-tuple-element.30.qh_ref, ...), custom_call_target="tpu_custom_call", output_to_operand_aliasing={{0}: (9, {}), {1}: (10, {})} | custom-call | flops 600000000 | bytes 3000000 | tf_op jit(solution)/shard_map/first/pallas_call | solution.py:470
  39.2 0.0 all-to-all-done.got_ref
  39.2 4.6 %total.1 = (f32[4,3,128,128]{3,2,1,0:T(8,128)}, f32[4,128,128]{2,1,0:T(8,128)}, f32[64,4,128]{2,1,0:T(4,128)}) custom-call(s32[1]{0:T(128)} %bitcast.idx_ref, f32[4,5,128,128]{3,2,1,0:T(8,128)} %get-tuple-element.36.raw_ref, bf16[16,512,128]{2,1,0:T(8,128)(2,1)} %get-tuple-element.31.ch_ref, f32[4,128,128]{2,1,0:T(8,128)} %get-tuple-element.37.nloc_ref, ...), custom_call_target="tpu_custom_call" | custom-call | flops 400000000 | bytes 2000000 | tf_op jit(solution)/shard_map/total/pallas_call | solution.py:482
  43.8 21.5 %all_to_all.30.got_ref = f32[64,4,128]{2,1,0:T(4,128)} all-to-all(f32[64,4,128]{2,1,0:T(4,128)} %get-tuple-element.43), channel_id=1, replica_groups=mesh['z'=8,'y'=4,'core'=2,'batch'=4] {'z','y','core'}, dimensions={0} | all-to-all | bytes 262144 | tf_op jit(solution)/shard_map/all_to_all | solution.py:419
  65.3 5.2 %state.1 = (f32[4,128,128]{2,1,0:T(8,128)}, f32[4,128,128]{2,1,0:T(8,128)}, f32[4,128,128]{2,1,0:T(8,128)}, f32[64,4,128]{2,1,0:T(4,128)}) custom-call(f32[4,5,128,128]{3,2,1,0:T(8,128)} %get-tuple-element.36.raw_ref, f32[4,3,128,128]{3,2,1,0:T(8,128)} %get-tuple-element.40.st_ref, bf16[16,512,128]{2,1,0:T(8,128)(2,1)} %get-tuple-element.31.ch_ref, ...), custom_call_target="tpu_custom_call" | custom-call | flops 400000000 | bytes 2000000 | tf_op jit(solution)/shard_map/state/pallas_call | solution.py:493
  70.5 5.2 %all-to-all-start.2 = ((f32[64,4,128]{2,1,0:T(4,128)}), f32[64,4,128]{2,1,0:T(4,128)}, u32[]{:S(2)}, u32[]{:S(2)}) async-start(f32[64,4,128]{2,1,0:T(4,128)} %get-tuple-element.51), calls=%async_computation.2 | async-start | bytes 262144 | tf_op jit(solution)/shard_map/all_to_all | solution.py:419
  75.8 6.4 %output.1 = (bf16[1,512,16,128]{3,2,1,0:T(8,128)(2,1)}, f32[128,128]{1,0:T(8,128)}) custom-call(f32[16,512,128]{2,1,0:T(8,128)} %get-tuple-element.35.numer_ref, f32[4,5,128,128]{3,2,1,0:T(8,128)} %get-tuple-element.36.raw_ref, f32[4,3,128,128]{3,2,1,0:T(8,128)} %get-tuple-element.40.st_ref, f32[4,128,128]{2,1,0:T(8,128)} %get-tuple-element.44.state_ref, ...), custom_call_target="tpu_custom_call" | custom-call | flops 800000000 | bytes 4000000 | tf_op jit(solution)/shard_map/output/pallas_call | solution.py:504
  82.2 4.7 %all-to-all-done.2.got_ref = f32[64,4,128]{2,1,0:T(4,128)} async-done(((f32[64,4,128]{2,1,0:T(4,128)}), f32[64,4,128]{2,1,0:T(4,128)}, u32[]{:S(2)}, u32[]{:S(2)}) %all-to-all-start.2) | async-done | bytes 131104 | tf_op jit(solution)/shard_map/all_to_all | solution.py:419
  86.9 5.9 %key_grad.1 = f32[256,128]{1,0:T(8,128)} custom-call(s32[1]{0:T(128)} %bitcast.idx_ref, bf16[16,512,128]{2,1,0:T(8,128)(2,1)} %get-tuple-element.28.kp_ref.ko_ref.kh_ref, bf16[16,512,128]{2,1,0:T(8,128)(2,1)} %get-tuple-element.29.vp_ref.vo_ref.vh_ref, f32[4,128,128]{2,1,0:T(8,128)} %get-tuple-element.47.sig_ref, ...), custom_call_target="tpu_custom_call" | custom-call | flops 600000000 | bytes 3000000 | tf_op jit(solution)/shard_map/key_grad/pallas_call | solution.py:513
  92.9 13.6 %all_to_all.31.x_ref = f32[16,16,128]{2,1,0:T(8,128)} all-to-all(f32[16,16,128]{2,1,0:T(8,128)} %bitcast.12), channel_id=1, replica_groups=mesh['z'=8,'y'=4,'core'=2,'batch'=4] {'z','core'}, dimensions={0} | all-to-all | bytes 262144 | tf_op jit(solution)/shard_map/all_to_all | solution.py:419
  106.4 1.6 %spread.2 = f32[16,16,128]{2,1,0:T(8,128)} custom-call(f32[16,16,128]{2,1,0:T(8,128)} %all_to_all.31.x_ref), custom_call_target="tpu_custom_call" | custom-call | flops 200000000 | bytes 1000000 | tf_op jit(solution)/shard_map/spread/pallas_call | solution.py:528
  108.0 12.1 %all_to_all.32.x_ref = f32[16,16,128]{2,1,0:T(8,128)} all-to-all(f32[16,16,128]{2,1,0:T(8,128)} %spread.2), channel_id=1, replica_groups=mesh['z'=8,'y'=4,'core'=2,'batch'=4] {'y','batch'}, dimensions={0} | all-to-all | bytes 262144 | tf_op jit(solution)/shard_map/all_to_all | solution.py:419
  120.1 1.6 %spread.3 = f32[16,16,128]{2,1,0:T(8,128)} custom-call(f32[16,16,128]{2,1,0:T(8,128)} %all_to_all.32.x_ref), custom_call_target="tpu_custom_call" | custom-call | flops 200000000 | bytes 1000000 | tf_op jit(solution)/shard_map/spread/pallas_call | solution.py:529
  121.7 13.5 %all_to_all.33 = f32[16,16,128]{2,1,0:T(8,128)S(1)} all-to-all(f32[16,16,128]{2,1,0:T(8,128)} %spread.3), channel_id=1, replica_groups=mesh['z'=8,'y'=4,'core'=2,'batch'=4] {'z','core'}, dimensions={0} | all-to-all | bytes 262144 | tf_op jit(solution)/shard_map/all_to_all | solution.py:419
  135.1 0.7 slice_bitcast_fusion
Async XLA Ops:
  7.4 26.8 %collective-permute-start = (bf16[2,16,128,128]{3,2,1,0:T(8,128)(2,1)}, bf16[2,16,128,128]{3,2,1,0:T(8,128)(2,1)}, u32[]{:S(2)}, u32[]{:S(2)}) collective-permute-start(bf16[2,16,128,128]{3,2,1,0:T(8,128)(2,1)} %get-tuple-element.32), channel_id=1, source_target_pairs={{0,4},{4,8},{8,12},{12,16},{16,20},{20,24},{24,28},{28,32},{32,36}... | collective-permute-start | bytes 3145736 | tf_op jit(solution)/shard_map/ppermute | solution.py:458
  12.0 27.1 %all-to-all-start = ((f32[64,4,128]{2,1,0:T(4,128)}), f32[64,4,128]{2,1,0:T(4,128)}, u32[]{:S(2)}, u32[]{:S(2)}) async-start(f32[64,4,128]{2,1,0:T(4,128)} %get-tuple-element.39), calls=%async_computation | async-start | bytes 262144 | tf_op jit(solution)/shard_map/all_to_all | solution.py:419
  70.5 16.4 %all-to-all-start.2 = ((f32[64,4,128]{2,1,0:T(4,128)}), f32[64,4,128]{2,1,0:T(4,128)}, u32[]{:S(2)}, u32[]{:S(2)}) async-start(f32[64,4,128]{2,1,0:T(4,128)} %get-tuple-element.51), calls=%async_computation.2 | async-start | bytes 262144 | tf_op jit(solution)/shard_map/all_to_all | solution.py:419

commit v2 on v1

--- a/solution.py
+++ b/solution.py
@@ -19,7 +19,7 @@
 SCALE = 1.0 / math.sqrt(DH)
 SCALE_LOG2 = SCALE * math.log2(math.e)
 NEG = -1e30
-VMEM = 67_043_328
+VMEM = 24 * 2**20
 F32 = jnp.float32
 BF16 = jnp.bfloat16
 NN = (((1,), (0,)), ((), ()))
@@ -75,18 +75,30 @@
     return jnp.broadcast_to(jnp.sum(x, 1, keepdims=True), (ROWS, TILE))
 
 
-def keys_kernel(idx_ref, cnt_ref, k_ref, v_ref, kmap_ref, kh_ref, vh_ref, halo_ref, local_ref,
+def keys_kernel(idx_ref, cnt_ref, k_ref, v_ref, kmap_ref, kh_ref, vh_ref, edge_ref, local_ref,
                 sig_ref, evict_ref, nloc_ref, msg_ref, pre, evict, st_all, st_ev, all_acc, nacc,
-                feats, msg):
+                feats, msg, kbuf, vbuf, ksem, vsem):
     n = pl.program_id(0)
 
+    def copies(m):
+        rows = pl.ds(m * TILE, TILE)
+        return (
+            pltpu.make_async_copy(k_ref.at[0, rows], kbuf.at[m], ksem.at[m]),
+            pltpu.make_async_copy(v_ref.at[0, rows], vbuf.at[m], vsem.at[m]),
+        )
+
     @pl.when(n == 0)
     def _():
+        for m in range(4):
+            for copy in copies(m):
+                copy.start()
         all_acc[...] = jnp.zeros_like(all_acc)
         nacc[...] = jnp.zeros_like(nacc)
 
-    kh_ref[...] = jnp.swapaxes(k_ref[0], 0, 1)
-    vh_ref[...] = jnp.swapaxes(v_ref[0], 0, 1)
+    for copy in copies(n):
+        copy.wait()
+    kh_ref[...] = jnp.swapaxes(kbuf[n], 0, 1)
+    vh_ref[...] = jnp.swapaxes(vbuf[n], 0, 1)
     lanes = lax.broadcasted_iota(jnp.int32, (RANK, TILE), 1)
     for h in range(HEADS):
         pre[of(h), :] = dot(kmap_ref[h], kh_ref[h], NT)
@@ -109,8 +121,8 @@
 
     @pl.when(n == 3)
     def _():
-        halo_ref[0] = kh_ref[...]
-        halo_ref[1] = vh_ref[...]
+        edge_ref[0] = kh_ref[...]
+        edge_ref[1] = vh_ref[...]
         row = row_sums(nacc[...] * (1.0 / 128.0))
         for s in range(64):
             msg[s, 0:2, :] = all_acc[2 * s : 2 * s + 2, :]
@@ -155,52 +167,17 @@
     raw_ref[0, 4] = cn[...]
 
 
-def near_kernel(idx_ref, cnt_ref, q_ref, c_ref, kp_ref, ko_ref, vp_ref, vo_ref, qmap_ref, qh_ref,
-                ch_ref, numer_ref, raw_ref, qs, cs, *scratch):
-    t = pl.program_id(0)
-    qs[...] = jnp.swapaxes(q_ref[0], 0, 1)
-    cs[...] = jnp.swapaxes(c_ref[0], 0, 1)
-
-    @pl.when(t > 0)
-    def _():
-        before = idx_ref[0] * 4 + jnp.maximum(t - 1, 0)
-        attention(kp_ref, ko_ref, vp_ref, vo_ref, qmap_ref, lambda h: cnt_ref[h, before], qs, cs,
-                  raw_ref, numer_ref, *scratch)
-
-    qh_ref[...] = qs[...]
-    ch_ref[...] = cs[...]
-
-
-def first_kernel(idx_ref, cnt_ref, qh_ref, ch_ref, halo_in, ko_ref, vo_ref, qmap_ref, kmap_ref,
-                 numer_any, raw_any, numer_ref, raw_ref, halo_ref, nhalo_ref, qs, cs, kept, feats,
-                 *scratch):
-    del numer_any, raw_any
-    index = idx_ref[0]
-    before = jnp.maximum(index * 4 - 1, 0)
-    pre = scratch[3]
-    lanes = lax.broadcasted_iota(jnp.int32, (RANK, TILE), 1)
-    counts = [jnp.where(index > 0, cnt_ref[h, before], 0) for h in range(HEADS)]
-    qs[...] = qh_ref[...]
-    cs[...] = ch_ref[...]
-    for h in range(HEADS):
-        pre[of(h), :] = dot(kmap_ref[h], halo_in[0, h], NT)
-        kept[of(h), :] = (lanes < counts[h]).astype(F32)
-    feat, sig = softplus_sigmoid(pre[...] - SHIFT)
-    feat = feat * kept[...]
-    feats[...] = feat
-    for h in range(HEADS):
-        feats[of(h), :] = folded(dot(stacked(feats[of(h), :]), halo_in[1, h]))
-    halo_ref[0] = feats[...]
-    halo_ref[1] = kept[...] * sig
-    nhalo_ref[...] = lane_sums(feat)
-    attention(halo_in.at[0], ko_ref, halo_in.at[1], vo_ref, qmap_ref, lambda h: counts[h], qs, cs,
-              raw_ref, numer_ref, *scratch)
-
-
-def total_kernel(idx_ref, raw_ref, ch_ref, nloc_ref, nhalo_ref, got_ref, st_ref, dst_ref, msg_ref,
-                 norm, norm_t, cf, dst, dacc, msg):
+def attend_kernel(idx_ref, cnt_ref, q_ref, c_ref, ko_ref, vo_ref, edge_ref, qmap_ref, kmap_ref,
+                  nloc_ref, got_ref, qh_ref, ch_ref, numer_ref, raw_ref, st_ref, dst_ref,
+                  halo_ref, msg_ref, qs, cs, kp, vp, kept, norm, norm_t, cf, dst, dacc, msg,
+                  *scratch):
     t = pl.program_id(0)
     index = idx_ref[0]
+    pre = scratch[3]
+    before = index * 4 + t - 1
+    counts = [
+        jnp.where(before >= 0, cnt_ref[h, jnp.maximum(before, 0)], 0) for h in range(HEADS)
+    ]
 
     @pl.when(t == 0)
     def _():
@@ -212,19 +189,40 @@
             run = run + got_ref[s, 0:2, :]
             nrun = nrun + jnp.where(s < index, got_ref[s, 2:3, :], 0.0)
         norm[...] = jnp.broadcast_to(nrun, (128, 128)).T
-        norm_t[...] = norm[...] - nhalo_ref[...]
+        kp[...] = edge_ref[0]
+        vp[...] = edge_ref[1]
+        lanes = lax.broadcasted_iota(jnp.int32, (RANK, TILE), 1)
+        for h in range(HEADS):
+            pre[of(h), :] = dot(kmap_ref[h], kp[h], NT)
+            kept[of(h), :] = (lanes < counts[h]).astype(F32)
+        feat, sig = softplus_sigmoid(pre[...] - SHIFT)
+        feat = feat * kept[...]
+        cf[...] = feat
+        for h in range(HEADS):
+            dst[of(h), :] = folded(dot(stacked(cf[of(h), :]), vp[h]))
+        halo_ref[0] = dst[...]
+        halo_ref[1] = kept[...] * sig
+        norm_t[...] = norm[...] - lane_sums(feat)
 
     @pl.when(t > 0)
     def _():
         norm_t[...] = norm[...] + nloc_ref[0]
 
+    qs[...] = jnp.swapaxes(q_ref[0], 0, 1)
+    cs[...] = jnp.swapaxes(c_ref[0], 0, 1)
+    attention(kp, ko_ref, vp, vo_ref, qmap_ref, lambda h: counts[h], qs, cs, raw_ref, numer_ref,
+              *scratch)
+    qh_ref[...] = qs[...]
+    ch_ref[...] = cs[...]
+    kp[...] = ko_ref[...]
+    vp[...] = vo_ref[...]
     feat = raw_ref[0, 0]
     decay = raw_ref[0, 2]
     rinv = 1.0 / (raw_ref[0, 3] + decay * per_head_sum(feat * norm_t[...]))
     coef = decay * rinv
     cf[...] = feat * coef
     for h in range(HEADS):
-        dst[of(h), :] = folded(dot(stacked(cf[of(h), :]), ch_ref[h]))
+        dst[of(h), :] = folded(dot(stacked(cf[of(h), :]), cs[h]))
     st_ref[0, 0] = coef
     st_ref[0, 1] = rinv
     st_ref[0, 2] = norm_t[...]
@@ -238,13 +236,15 @@
         msg_ref[...] = msg[...]
 
 
-def state_kernel(raw_ref, st_ref, ch_ref, local_ref, halo_ref, got_ref, state_ref, pre_ref, dn_ref,
-                 msg_ref, far, state, grad, drow, msg):
+def output_kernel(numer_ref, raw_ref, st_ref, qh_ref, ch_ref, local_ref, halo_ref, got_ref,
+                  out_ref, gq_ref, dn_ref, msg_ref, far, state, grad, drow, msg, cf, rinv, out,
+                  gq):
     t = pl.program_id(0)
 
     @pl.when(t == 0)
     def _():
         drow[...] = jnp.zeros_like(drow)
+        gq[...] = jnp.zeros_like(gq)
         run = jnp.zeros((2, 128), F32)
         for s in reversed(range(64)):
             far[2 * s : 2 * s + 2, :] = got_ref[s, 0:2, :]
@@ -256,36 +256,9 @@
     def _():
         state[...] = far[...] + local_ref[0]
 
-    for h in range(HEADS):
-        grad[of(h), :] = folded(dot(stacked(state[of(h), :]), ch_ref[h], NT))
-    state_ref[0] = state[...]
     coef = st_ref[0, 0]
-    cf = raw_ref[0, 0] * coef
-    along = raw_ref[0, 4] * st_ref[0, 1] + per_head_sum(cf * grad[...])
-    pre_ref[0] = coef * (grad[...] - along * st_ref[0, 2]) * raw_ref[0, 1]
-    dn = -(cf * along)
-    dn_ref[0] = lane_sums(dn)
-    drow[...] += row_sums(dn)
-
-    @pl.when(t == 3)
-    def _():
-        for s in range(64):
-            msg[s, 2:4, :] = drow[0:2, :]
-        msg_ref[...] = msg[...]
-
-
-def output_kernel(numer_ref, raw_ref, st_ref, state_ref, pre_ref, qh_ref, out_ref, gq_ref, cf,
-                  rinv, state, pre, out, gq):
-    t = pl.program_id(0)
-
-    @pl.when(t == 0)
-    def _():
-        gq[...] = jnp.zeros_like(gq)
-
-    cf[...] = raw_ref[0, 0] * st_ref[0, 0]
+    cf[...] = raw_ref[0, 0] * coef
     rinv[...] = st_ref[0, 1]
-    state[...] = state_ref[0]
-    pre[...] = pre_ref[0]
     sub = lax.broadcasted_iota(jnp.int32, (RANK, TILE), 0)
     ones = jnp.ones((RANK, DH), F32)
     zeros = jnp.zeros((RANK, DH), F32)
@@ -300,17 +273,27 @@
         r_mid = (r - r_hi).astype(BF16).astype(F32)
         pieces = jnp.where(sub == 0, r_hi, jnp.where(sub == 1, r_mid, r - r_hi - r_mid))
         pieces = jnp.where(sub < 3, pieces, 0.0)
+        grad[of(h), :] = folded(dot(stacked(s), ch_ref[h], NT))
         lhs = jnp.concatenate([c_hi, c - c_hi, c_hi, pieces], 0).astype(BF16)
         left = jnp.concatenate([s_hi, s_hi, s_lo, zeros], 0)
         right = jnp.concatenate([zeros, zeros, zeros, ones], 0)
         both = dot(lhs, jnp.concatenate([left, right], 1).astype(BF16), TN)
         out[h] = (numer_ref[h] * both[:, DH:] + both[:, :DH]).astype(BF16)
-        gq[of(h), :] += folded(dot(stacked(pre[of(h), :]), qh_ref[h]))
+    along = raw_ref[0, 4] * rinv[...] + per_head_sum(cf[...] * grad[...])
+    dn = -(cf[...] * along)
+    grad[...] = coef * (grad[...] - along * st_ref[0, 2]) * raw_ref[0, 1]
+    for h in range(HEADS):
+        gq[of(h), :] += folded(dot(stacked(grad[of(h), :]), qh_ref[h]))
     out_ref[0] = jnp.swapaxes(out[...], 0, 1)
+    dn_ref[0] = lane_sums(dn)
+    drow[...] += row_sums(dn)
 
     @pl.when(t == 3)
     def _():
         gq_ref[...] = gq[...]
+        for s in range(64):
+            msg[s, 2:4, :] = drow[0:2, :]
+        msg_ref[...] = msg[...]
 
 
 def key_grad_kernel(idx_ref, kh_ref, vh_ref, sig_ref, evict_ref, dst_ref, dn_ref, halo_in,
@@ -382,10 +365,6 @@
     return t
 
 
-def first(t):
-    return 0
-
-
 def prev(t):
     return jnp.maximum(t - 1, 0)
 
@@ -395,7 +374,8 @@
 
 
 SMEM = pl.BlockSpec(memory_space=pltpu.SMEM)
-ANY = pl.BlockSpec(memory_space=pl.ANY)
+HBM = pl.BlockSpec(memory_space=pltpu.HBM)
+TILES_S = pltpu.VMEM((4, TILE, HEADS, DH), BF16)
 MAPS = whole(HEADS, RANK, DH)
 MSG = whole(64, 4, 128)
 MSG_T = sds((64, 4, 128))
@@ -419,7 +399,7 @@
     return lax.all_to_all(x, axes, split_axis=0, concat_axis=0, tiled=True)
 
 
-def call(kernel, name, grid, in_specs, out_specs, out_shape, scratch, us, aliases=None):
+def call(kernel, name, grid, in_specs, out_specs, out_shape, scratch, us):
     return pl.pallas_call(
         kernel,
         grid=(grid,),
@@ -428,7 +408,6 @@
         out_shape=out_shape,
         scratch_shapes=scratch,
         name=name,
-        input_output_aliases=aliases or {},
         cost_estimate=pl.CostEstimate(
             flops=int(us * 2e8), bytes_accessed=int(us * 1e6), transcendentals=0
         ),
@@ -448,67 +427,42 @@
 
     kh, vh, edge, local, sig_k, evict, nloc, msg = call(
         keys_kernel, "keys", 4,
-        [SMEM, SMEM, NAT, NAT, MAPS],
+        [SMEM, SMEM, HBM, HBM, MAPS],
         [by_head(same), by_head(same), HALO, part(same), part(same), part(same), part(same), MSG],
         [BIG, BIG, sds((2, HEADS, TILE, DH), BF16), PARTS, PARTS, PARTS, PARTS, MSG_T],
-        [SQ, SQ, SQ, SQ, SQ, SQ, pltpu.VMEM((2, ROWS, TILE), F32), MSG_S],
+        [SQ, SQ, SQ, SQ, SQ, SQ, pltpu.VMEM((2, ROWS, TILE), F32), MSG_S,
+         TILES_S, TILES_S, pltpu.SemaphoreType.DMA((4,)), pltpu.SemaphoreType.DMA((4,))],
         4,
     )(index, counts, keys, values, kmap)
 
-    halo_kv = lax.ppermute(edge, SEQ, steps)
+    edge = lax.ppermute(edge, SEQ, steps)
     got = exchanged(msg, SEQ)
 
-    qh, ch, numer, raw = call(
-        near_kernel, "near", 4,
-        [SMEM, SMEM, NAT, NAT, by_head(prev), by_head(same), by_head(prev), by_head(same), MAPS],
-        [by_head(same), by_head(same), by_head(same), part(same, 5)],
-        [BIG, BIG, sds((HEADS, 4 * TILE, DH)), sds((4, 5, ROWS, TILE))],
-        [HEAD_S, HEAD_S, *ATTEND_S],
-        8,
-    )(index, counts, queries, cotangent, kh, kh, vh, vh, qmap)
-
-    numer, raw, halo, nhalo = call(
-        first_kernel, "first", 1,
-        [SMEM, SMEM, by_head(first), by_head(first), HALO, by_head(first), by_head(first), MAPS,
-         MAPS, ANY, ANY],
-        [by_head(first), part(first, 5), PAIR, whole(ROWS, TILE)],
-        [sds((HEADS, 4 * TILE, DH)), sds((4, 5, ROWS, TILE)), sds((2, ROWS, TILE)),
-         sds((ROWS, TILE))],
-        [HEAD_S, HEAD_S, SQ, SQ, *ATTEND_S],
-        3,
-        {9: 0, 10: 1},
-    )(index, counts, qh, ch, halo_kv, kh, vh, qmap, kmap, numer, raw)
-
-    st, dst, msg = call(
-        total_kernel, "total", 4,
-        [SMEM, part(same, 5), by_head(same), part(prev), whole(ROWS, TILE), MSG],
-        [part(same, 3), part(same), MSG],
-        [sds((4, 3, ROWS, TILE)), PARTS, MSG_T],
-        [SQ, SQ, SQ, SQ, SQ, MSG_S],
-        2,
-    )(index, raw, ch, nloc, nhalo, got)
+    qh, ch, numer, raw, st, dst, halo, msg = call(
+        attend_kernel, "attend", 4,
+        [SMEM, SMEM, NAT, NAT, by_head(same), by_head(same), HALO, MAPS, MAPS,
+         part(prev), MSG],
+        [by_head(same), by_head(same), by_head(same), part(same, 5), part(same, 3), part(same),
+         PAIR, MSG],
+        [BIG, BIG, sds((HEADS, 4 * TILE, DH)), sds((4, 5, ROWS, TILE)), sds((4, 3, ROWS, TILE)),
+         PARTS, sds((2, ROWS, TILE)), MSG_T],
+        [HEAD_S, HEAD_S, HEAD_S, HEAD_S, SQ, SQ, SQ, SQ, SQ, SQ, MSG_S, *ATTEND_S],
+        10,
+    )(index, counts, queries, cotangent, kh, vh, edge, qmap, kmap, nloc, got)
 
     got = exchanged(msg, SEQ)
 
-    state, pre_q, dn, msg = call(
-        state_kernel, "state", 4,
-        [part(same, 5), part(same, 3), by_head(same), part(prev), PAIR, MSG],
-        [part(same), part(same), part(same), MSG],
-        [PARTS, PARTS, PARTS, MSG_T],
-        [SQ, SQ, SQ, pltpu.VMEM((8, 128), F32), MSG_S],
-        2,
-    )(raw, st, ch, local, halo, got)
+    out, gq, dn, msg = call(
+        output_kernel, "output", 4,
+        [by_head(same), part(same, 5), part(same, 3), by_head(same), by_head(same), part(prev),
+         PAIR, MSG],
+        [NAT, whole(ROWS, TILE), part(same), MSG],
+        [sds((1, 4 * TILE, HEADS, DH), BF16), sds((ROWS, TILE)), PARTS, MSG_T],
+        [SQ, SQ, SQ, pltpu.VMEM((8, 128), F32), MSG_S, SQ, SQ, HEAD_S, SQ],
+        5,
+    )(numer, raw, st, qh, ch, local, halo, got)
 
     got = exchanged(msg, SEQ)
-
-    out, gq = call(
-        output_kernel, "output", 4,
-        [by_head(same), part(same, 5), part(same, 3), part(same), part(same), by_head(same)],
-        [NAT, whole(ROWS, TILE)],
-        [sds((1, 4 * TILE, HEADS, DH), BF16), sds((ROWS, TILE))],
-        [SQ, SQ, SQ, SQ, HEAD_S, SQ],
-        4,
-    )(numer, raw, st, state, pre_q, qh)
 
     grads = call(
         key_grad_kernel, "key_grad", 4,
@@ -518,7 +472,7 @@
         sds((2 * ROWS, TILE)),
         [SQ, SQ, SQ, SQ, SQ, SQ],
         3,
-    )(index, kh, vh, sig_k, evict, dst, dn, halo_kv, halo, got, gq)
+    )(index, kh, vh, sig_k, evict, dst, dn, edge, halo, got, gq)
 
     spread = call(
         spread_kernel, "spread", 1, [whole(16, 16, 128)], whole(16, 16, 128), sds((16, 16, 128)),

time: 137 us -> 126 us (0.920)
  blocking collectives: 60.6 us -> 91.2 us
  Pallas kernels: 47.6 us -> 23.8 us
  starting transfers between devices: 21.5 us -> 4.58 us
  waiting for transfers between devices: 4.73 us -> 0.01 us
  local copies, waits for them, and re-layouts: 0.66 us -> 5.32 us
    all_to_all x4 -> x6, blocking collectives: 60.6 us -> 91.2 us  [exchanged(): return lax.all_to_all(x, axes, split_axis=0, concat_axis=0, tiled=True)]
    all_to_all x2 -> x0, starting transfers between devices: 16.9 us -> none  [exchanged(): return lax.all_to_all(x, axes, split_axis=0, concat_axis=0, tiled=True)]
    pallas_call x5 -> x2, Pallas kernels: 32.1 us -> 15.8 us  [the longest x1 11.6 us: body(): call(attend_kernel, 'attend', 4, [SMEM, SMEM, NAT, NAT, by_head(same), by...]
    all_to_all x2 -> x0, waiting for transfers between devices: 4.73 us -> none  [exchanged(): return lax.all_to_all(x, axes, split_axis=0, concat_axis=0, tiled=True)]
    unnamed x0 -> x14, local copies, waits for them, and re-layouts: none -> 4.66 us
    pallas_call x1, Pallas kernels: 5.94 us -> 3.01 us  [body(): call(key_grad_kernel, 'key_grad', 4, [SMEM, by_head(back), by_head(back),...]
    pallas_call x1, Pallas kernels: 6.43 us -> 4.87 us  [body(): call(output_kernel, 'output', 4, [by_head(same), part(same, 5), part(same...]
    pallas_call x1, Pallas kernels: 1.58 us -> 0.03 us  [body(): grads = exchanged(spread(grads), ('y', 'batch'))]
  transfers between devices with their start and end apart: 3 -> 1, of which waited for: 1 -> 0; matrix products, arithmetic and copies ran while one was open for 0% -> 0% of each run, Pallas kernels for 16% -> 0%
where the time goes in v2:
time: 126 us
  blocking collectives  91.2 us (72%)
  Pallas kernels  23.8 us (19%)
  local copies, waits for them, and re-layouts  5.32 us (4%)
  starting transfers between devices  4.58 us (4%)
    all_to_all x6, blocking collectives, exchanged(): return lax.all_to_all(x, axes, split_axis=0, concat_axis=0, tiled=True)  91.2 us
    pallas_call x1, Pallas kernels, body(): call(attend_kernel, 'attend', 4, [SMEM, SMEM, NAT, NAT, by_head(same), by...  11.6 us
    pallas_call x1, Pallas kernels, body(): call(output_kernel, 'output', 4, [by_head(same), part(same, 5), part(same...  4.87 us
    unnamed x14, local copies, waits for them, and re-layouts  4.66 us
    ppermute x1, starting transfers between devices, body(): edge = lax.ppermute(edge, SEQ, steps)  4.58 us
    pallas_call x1, Pallas kernels, body(): call(keys_kernel, 'keys', 4, [SMEM, SMEM, HBM, HBM, MAPS], [by_head(same)...  4.19 us
    pallas_call x1, Pallas kernels, body(): call(key_grad_kernel, 'key_grad', 4, [SMEM, by_head(back), by_head(back),...  3.01 us
  transfers between devices with their start and end apart: 1, of which 0 were waited for; matrix products, arithmetic and copies ran while one was open for 0% of the time, Pallas kernels for 0%

profile of v2, /device:TPU:1, one launch (start us, length us, event | category | flops | bytes accessed | tf_op | source)
XLA Modules:
  0.0 125.5 jit_solution(7109668893138209218)
XLA Ops:
  0.6 0.0 copy-start.2
  0.7 1.6 %copy-done.2 = bf16[1,512,16,128]{3,2,1,0:T(8,128)(2,1)S(1)} copy-done((bf16[1,512,16,128]{3,2,1,0:T(8,128)(2,1)S(1)}, bf16[1,512,16,128]{3,2,1,0:T(8,128)(2,1)}, u32[]{:S(2)}) %copy-start.2) | copy-done | bytes 2097176
  2.2 0.0 copy-start.3
  2.2 1.6 %copy-done.3 = bf16[1,512,16,128]{3,2,1,0:T(8,128)(2,1)S(1)} copy-done((bf16[1,512,16,128]{3,2,1,0:T(8,128)(2,1)S(1)}, bf16[1,512,16,128]{3,2,1,0:T(8,128)(2,1)}, u32[]{:S(2)}) %copy-start.3) | copy-done | bytes 2097176
  3.8 0.0 copy-start.4
  3.8 0.8 copy-done.4
  4.6 0.0 copy-start.5
  4.6 0.7 copy-done.5
  5.3 4.2 %keys.1 = (bf16[16,512,128]{2,1,0:T(8,128)(2,1)S(1)}, bf16[16,512,128]{2,1,0:T(8,128)(2,1)S(1)}, bf16[2,16,128,128]{3,2,1,0:T(8,128)(2,1)S(1)}, f32[4,128,128]{2...) custom-call(s32[1]{0:T(128)} %bitcast.idx_ref, ...), custom_call_target="tpu_custom_call" | custom-call | flops 800000000 | bytes 4000000 | tf_op jit(solution)/shard_map/keys/pallas_call | solution.py:428
  9.5 4.6 %collective-permute-start = (bf16[2,16,128,128]{3,2,1,0:T(8,128)(2,1)S(1)}, bf16[2,16,128,128]{3,2,1,0:T(8,128)(2,1)S(1)}, u32[]{:S(2)}, u32[]{:S(2)}) collective-permute-start(bf16[2,16,128,128]{3,2,1,0:T(8,128)(2,1)S(1)} %get-tuple-element.25), channel_id=1, source_target_pairs={{0,4},{4,8},{8,12},{12,16},{16,20},{20,24},{24,28},{28,32},{32,36}... | collective-permute-start | bytes 3145736 | tf_op jit(solution)/shard_map/ppermute | solution.py:438
  14.1 22.5 %all_to_all.30.got_ref = f32[64,4,128]{2,1,0:T(4,128)S(1)} all-to-all(f32[64,4,128]{2,1,0:T(4,128)S(1)} %get-tuple-element.27), channel_id=1, replica_groups=mesh['z'=8,'y'=4,'core'=2,'batch'=4] {'z','y','core'}, dimensions={0} | all-to-all | bytes 262144 | tf_op jit(solution)/shard_map/all_to_all | solution.py:399
  36.6 0.0 collective-permute-done.edge_ref.halo_in
  36.6 0.0 copy-done
  36.6 0.0 copy-done.1
  36.6 0.0 copy-done.6
  36.6 11.6 %attend.1 = (bf16[16,512,128]{2,1,0:T(8,128)(2,1)S(1)}, bf16[16,512,128]{2,1,0:T(8,128)(2,1)S(1)}, f32[16,512,128]{2,1,0:T(8,128)S(1)}, f32[4,5,128,128]{3,2,1,0...) custom-call(s32[1]{0:T(128)} %bitcast.idx_ref, ...), custom_call_target="tpu_custom_call" | custom-call | flops 2000000000 | bytes 10000000 | tf_op jit(solution)/shard_map/attend/pallas_call | solution.py:441
  48.3 17.4 %all_to_all.31.got_ref = f32[64,4,128]{2,1,0:T(4,128)S(1)} all-to-all(f32[64,4,128]{2,1,0:T(4,128)S(1)} %get-tuple-element.35), channel_id=1, replica_groups=mesh['z'=8,'y'=4,'core'=2,'batch'=4] {'z','y','core'}, dimensions={0} | all-to-all | bytes 262144 | tf_op jit(solution)/shard_map/all_to_all | solution.py:399
  65.7 4.9 %output.1 = (bf16[1,512,16,128]{3,2,1,0:T(8,128)(2,1)}, f32[128,128]{1,0:T(8,128)S(1)}, f32[4,128,128]{2,1,0:T(8,128)S(1)}, f32[64,4,128]{2,1,0:T(4,128)S(1)}) custom-call(f32[16,512,128]{2,1,0:T(8,128)S(1)} %get-tuple-element.28.numer_ref, f32[4,5,128,128]{3,2,1,0:T(8,128)S(1)} %get-tuple-element.29.raw_ref, ...), custom_call_target="tpu_custom_call" | custom-call | flops 1000000000 | bytes 5000000 | tf_op jit(solution)/shard_map/output/pallas_call | solution.py:455
  70.5 14.9 %all_to_all.32.got_ref = f32[64,4,128]{2,1,0:T(4,128)S(1)} all-to-all(f32[64,4,128]{2,1,0:T(4,128)S(1)} %get-tuple-element.41), channel_id=1, replica_groups=mesh['z'=8,'y'=4,'core'=2,'batch'=4] {'z','y','core'}, dimensions={0} | all-to-all | bytes 262144 | tf_op jit(solution)/shard_map/all_to_all | solution.py:399
  85.4 3.0 %key_grad.1 = f32[256,128]{1,0:T(8,128)S(1)} custom-call(s32[1]{0:T(128)} %bitcast.idx_ref, bf16[16,512,128]{2,1,0:T(8,128)(2,1)S(1)} %get-tuple-element.23.ko_ref.kh_ref, bf16[16,512,128]{2,1,0:T(8,128)(2,1)S(1)} %get-tuple-element.24.vo_ref.vh_ref, f32[4,128,128]{2,1,0:T(8,128)S(1)} %get-tuple-element.37.sig_ref, ...), custom_call_target="tpu_custom_call" | custom-call | flops 600000000 | bytes 3000000 | tf_op jit(solution)/shard_map/key_grad/pallas_call | solution.py:467
  88.4 12.0 %all_to_all.33.x_ref = f32[16,16,128]{2,1,0:T(8,128)S(1)} all-to-all(f32[16,16,128]{2,1,0:T(8,128)S(1)} %bitcast.12), channel_id=1, replica_groups=mesh['z'=8,'y'=4,'core'=2,'batch'=4] {'z','core'}, dimensions={0} | all-to-all | bytes 262144 | tf_op jit(solution)/shard_map/all_to_all | solution.py:399
  100.5 12.2 %all_to_all.34.x_ref = f32[16,16,128]{2,1,0:T(8,128)S(1)} all-to-all(f32[16,16,128]{2,1,0:T(8,128)S(1)} %spread.2), channel_id=1, replica_groups=mesh['z'=8,'y'=4,'core'=2,'batch'=4] {'y','batch'}, dimensions={0} | all-to-all | bytes 262144 | tf_op jit(solution)/shard_map/all_to_all | solution.py:399
  112.7 12.2 %all_to_all.35 = f32[16,16,128]{2,1,0:T(8,128)S(1)} all-to-all(f32[16,16,128]{2,1,0:T(8,128)S(1)} %spread.3), channel_id=1, replica_groups=mesh['z'=8,'y'=4,'core'=2,'batch'=4] {'z','core'}, dimensions={0} | all-to-all | bytes 262144 | tf_op jit(solution)/shard_map/all_to_all | solution.py:399
  124.9 0.7 slice_bitcast_fusion
  (5 shorter events, 0.1 us)
Async XLA Ops:
  0.6 1.6 %copy-start.2 = (bf16[1,512,16,128]{3,2,1,0:T(8,128)(2,1)S(1)}, bf16[1,512,16,128]{3,2,1,0:T(8,128)(2,1)}, u32[]{:S(2)}) copy-start(bf16[1,512,16,128]{3,2,1,0:T(8,128)(2,1)} %k_ref.1) | copy-start | bytes 6291460
  2.2 1.6 %copy-start.3 = (bf16[1,512,16,128]{3,2,1,0:T(8,128)(2,1)S(1)}, bf16[1,512,16,128]{3,2,1,0:T(8,128)(2,1)}, u32[]{:S(2)}) copy-start(bf16[1,512,16,128]{3,2,1,0:T(8,128)(2,1)} %v_ref.1) | copy-start | bytes 6291460
  3.8 0.8 copy-start.4
  4.6 0.7 copy-start.5
  5.3 31.3 %copy-start = (bf16[1,512,16,128]{3,2,1,0:T(8,128)(2,1)S(1)}, bf16[1,512,16,128]{3,2,1,0:T(8,128)(2,1)}, u32[]{:S(2)}) copy-start(bf16[1,512,16,128]{3,2,1,0:T(8,128)(2,1)} %q_ref.1) | copy-start | bytes 6291460
  5.3 31.3 %copy-start.1 = (bf16[1,512,16,128]{3,2,1,0:T(8,128)(2,1)S(1)}, bf16[1,512,16,128]{3,2,1,0:T(8,128)(2,1)}, u32[]{:S(2)}) copy-start(bf16[1,512,16,128]{3,2,1,0:T(8,128)(2,1)} %c_ref.1) | copy-start | bytes 6291460
  5.3 31.3 %copy-start.6 = (bf16[16,128,8]{1,2,0:T(8,128)(2,1)S(1)}, bf16[16,128,8]{1,2,0:T(8,128)(2,1)}, u32[]{:S(2)}) copy-start(bf16[16,128,8]{1,2,0:T(8,128)(2,1)} %param.11) | copy-start | bytes 98308
  9.5 27.1 %collective-permute-start = (bf16[2,16,128,128]{3,2,1,0:T(8,128)(2,1)S(1)}, bf16[2,16,128,128]{3,2,1,0:T(8,128)(2,1)S(1)}, u32[]{:S(2)}, u32[]{:S(2)}) collective-permute-start(bf16[2,16,128,128]{3,2,1,0:T(8,128)(2,1)S(1)} %get-tuple-element.25), channel_id=1, source_target_pairs={{0,4},{4,8},{8,12},{12,16},{16,20},{20,24},{24,28},{28,32},{32,36}... | collective-permute-start | bytes 3145736 | tf_op jit(solution)/shard_map/ppermute | solution.py:438
